TPU v7x, 32 devices: a whole 2x2x4 slice. The times are simulated.
32 devices in a mesh: fsdp: 16 (over z, x, core), tensor: 2 (over y).
Axes of the slice: x: 2, y: 2, z: 4, core: 2. Of those that a mesh axis runs over, the one named last changes fastest.
Arguments:
- tokens: bfloat16 [4096, 2048], P('fsdp'), may hold values from -6 to 6
- grad_out: bfloat16 [4096, 2048], P('fsdp'), may hold values from -6 to 6
- segments: int32 [32, 128], P('fsdp'), may hold values from 0 to 3, as said below
- attention_gain: float32 [2048], P('fsdp'), may hold values from 0.5 to 1.5
- query_weight: bfloat16 [2048, 2048], P('fsdp', 'tensor'), may hold values from -0.125 to 0.125
- key_weight: bfloat16 [2048, 1024], P('fsdp', 'tensor'), may hold values from -0.125 to 0.125
- value_weight: bfloat16 [2048, 1024], P('fsdp', 'tensor'), may hold values from -0.125 to 0.125
- output_weight: bfloat16 [2048, 2048], P('tensor', 'fsdp'), may hold values from -0.5 to 0.5
- query_gain: float32 [128], replicated, may hold values from 0.5 to 1.5
- key_gain: float32 [128], replicated, may hold values from 0.5 to 1.5
- feedforward_gain: float32 [2048], P('fsdp'), may hold values from 0.5 to 1.5
- gate_weight: bfloat16 [2048, 6144], P('fsdp', 'tensor'), may hold values from -0.125 to 0.125
- up_weight: bfloat16 [2048, 6144], P('fsdp', 'tensor'), may hold values from -0.125 to 0.125
- down_weight: bfloat16 [6144, 2048], P('tensor', 'fsdp'), may hold values from -0.078125 to 0.078125
Outputs:
- mixed: bfloat16 [4096, 2048], P('fsdp')
- grad_tokens: float32 [4096, 2048], P('fsdp')
- grad_attention_gain: float32 [2048], P('fsdp')
- grad_query_weight: float32 [2048, 2048], P('fsdp', 'tensor')
- grad_key_weight: float32 [2048, 1024], P('fsdp', 'tensor')
- grad_value_weight: float32 [2048, 1024], P('fsdp', 'tensor')
- grad_output_weight: float32 [2048, 2048], P('tensor', 'fsdp')
- grad_query_gain: float32 [128], replicated
- grad_key_gain: float32 [128], replicated
- grad_feedforward_gain: float32 [2048], P('fsdp')
- grad_gate_weight: float32 [2048, 6144], P('fsdp', 'tensor')
- grad_up_weight: float32 [2048, 6144], P('fsdp', 'tensor')
- grad_down_weight: float32 [6144, 2048], P('tensor', 'fsdp')
Inputs may be any that keep to these rules, and one draw needn't show every extreme that they name: `segments`: segment numbers never fall along a row; every row holds one or more whole sequences, and some row is a single sequence of 128 tokens.
All inputs are finite; a program needn't handle non-finite values.
Results may differ from a plain program's by a relative error of at most 0.035.
Values may be sent and summed in bfloat16 or wider, within the bound.
A program may use at most 256 MiB of HBM per device.

v0:
```python
import functools

import jax
import jax.numpy as jnp
from jax import lax
from jax.experimental import pallas as pl
from jax.experimental.pallas import tpu as pltpu
from jax.sharding import Mesh
from jax.sharding import PartitionSpec as P


epsilon = 1e-06
rope_base = 1000000.0
bf16 = jnp.bfloat16
f32 = jnp.float32
MESH = pl.DeviceIdType.MESH
chunk = 16
vmem_limit = 40 * 1024 * 1024

bits = {"core": 4, "x": 2, "y": 1}
orders = (("x", "y", "core"), ("y", "x", "core"))
layer = [("core", 1), ("x", 1), ("y", 1)]


def normalize(values):
    inverse = lax.rsqrt(jnp.mean(values * values, axis=-1, keepdims=True) + epsilon)
    return values * inverse, inverse


def norm_back(upstream, normed, inverse):
    return inverse * (upstream - normed * jnp.mean(upstream * normed, axis=-1, keepdims=True))


def dot(left, right):
    return jnp.dot(left, right, preferred_element_type=f32)


def dot_tn(left, right):
    return lax.dot_general(left, right, (((0,), (0,)), ((), ())), preferred_element_type=f32)


def dot_nt(left, right):
    return lax.dot_general(left, right, (((1,), (1,)), ((), ())), preferred_element_type=f32)


def parts_of(width, count):
    tiles = width // 128
    edges = [i * (tiles // count) * 128 for i in range(count)] + [width]
    return [pl.ds(edges[i], edges[i + 1] - edges[i]) for i in range(count)]


def neighbour(axis, step=1):
    return {axis: lax.axis_index(axis) ^ step}


def square_id(step):
    return {"x": lax.axis_index("x") ^ (step >> 1), "core": lax.axis_index("core") ^ (step & 1)}


def square_place(step):
    device = square_id(step)
    return device["x"] * 2 + device["core"]


square = [("core", 1), ("x", 1), ("both", 0)]


def greet(axes):
    barrier = pltpu.get_barrier_semaphore()
    for axis in axes:
        device = square_id(3) if axis[0] == "both" else neighbour(*axis)
        pl.semaphore_signal(barrier, inc=1, device_id=device, device_id_type=MESH)
    pl.semaphore_wait(barrier, len(axes))


def copy_to(device, source, target, sems, number):
    return pltpu.make_async_remote_copy(
        src_ref=source,
        dst_ref=target,
        send_sem=sems[0].at[number],
        recv_sem=sems[1].at[number],
        device_id=device,
        device_id_type=MESH,
    )


def sem_pair(count):
    return [pltpu.SemaphoreType.DMA((count,)), pltpu.SemaphoreType.DMA((count,))]


def over_rows(rows, body):
    def step(i, carry):
        body(pl.ds(pl.multiple_of(i * chunk, chunk), chunk))
        return carry

    lax.fori_loop(0, rows // chunk, step, 0)


def gather_blocks(blocks, sems):
    gather_finish(*gather_start(blocks, sems))


def gather_start(blocks, sems):
    parts = parts_of(blocks.shape[2], len(orders))
    copies = {}

    def send(p, axis, i):
        copies[p, axis, i] = copy_to(
            neighbour(axis),
            blocks.at[i, :, parts[p]],
            blocks.at[i ^ bits[axis], :, parts[p]],
            sems,
            len(copies),
        )
        copies[p, axis, i].start()

    for place in range(3):
        for p, order in enumerate(orders):
            send(p, order[place], 0)
    return copies, send


def gather_finish(copies, send):
    for p, (a, b, c) in enumerate(orders):
        copies[p, a, 0].wait_recv()
        send(p, b, bits[a])
        send(p, c, bits[a])
    for p, (a, b, c) in enumerate(orders):
        copies[p, b, 0].wait_recv()
        send(p, c, bits[b])
        copies[p, b, bits[a]].wait_recv()
        send(p, c, bits[a] ^ bits[b])
    for p, (a, b, c) in enumerate(orders):
        for i in (0, bits[a], bits[b], bits[a] ^ bits[b]):
            copies[p, c, i].wait_recv()
    for copy in copies.values():
        copy.wait_send()


class Scatter:
    def __init__(self, blocks, scratch):
        self.blocks = blocks
        self.first, self.second, self.third, self.sent = scratch[:4]
        self.sems = scratch[4:6]
        self.parts = parts_of(blocks.shape[2], len(orders))
        self.copies = []
        self.arrive = {}

    def send(self, axis, source, target):
        self.copies.append(
            copy_to(neighbour(axis), source, target, self.sems, len(self.copies))
        )
        self.copies[-1].start()
        return self.copies[-1]

    def ready(self, i):
        for p, (a, b, c) in enumerate(orders):
            if i & bits[c]:
                k = (1 if i & bits[a] else 0) + (2 if i & bits[b] else 0)
                self.arrive[p, k] = self.send(
                    c, self.blocks.at[i, :, self.parts[p]], self.first.at[k, :, self.parts[p]]
                )

    def steps(self):
        rows = self.blocks.shape[1]
        blocks, first, second, sent = self.blocks, self.first, self.second, self.sent
        for k in (3, 2):
            for p, (a, b, c) in enumerate(orders):
                j = (bits[a] if k & 1 else 0) ^ bits[b]
                part = self.parts[p]
                self.arrive[p, k].wait_recv()

                def add(row, j=j, k=k, part=part):
                    value = blocks[j, row, part].astype(f32) + first[k, row, part].astype(f32)
                    sent[k - 1, row, part] = value.astype(bf16)

                over_rows(rows, add)
                self.arrive[p, k + 2] = self.send(
                    b, sent.at[k - 1, :, part], second.at[k - 2, :, part]
                )
                yield
        for p, (a, b, c) in enumerate(orders):
            part = self.parts[p]
            self.arrive[p, 1].wait_recv()
            self.arrive[p, 5].wait_recv()

            def add(row, j=bits[a], part=part):
                value = blocks[j, row, part].astype(f32) + first[1, row, part].astype(f32)
                value = value + second[1, row, part].astype(f32)
                sent[0, row, part] = value.astype(bf16)

            over_rows(rows, add)
            self.arrive[p, 6] = self.send(a, sent.at[0, :, part], self.third.at[0, :, part])
            yield
        for p in range(len(orders)):
            for k in (0, 4, 6):
                self.arrive[p, k].wait_recv()
        for copy in self.copies:
            copy.wait_send()

    def run(self):
        for _ in self.steps():
            pass

    def row(self, row):
        value = self.blocks[0, row].astype(f32) + self.first[0, row].astype(f32)
        return value + self.second[0, row].astype(f32) + self.third[0, row].astype(f32)


block_order = (7, 6, 5, 3, 4, 2, 1, 0)


def scatter_scratch(rows, width):
    return [
        pltpu.VMEM((4, rows, width), bf16),
        pltpu.VMEM((2, rows, width), bf16),
        pltpu.VMEM((1, rows, width), bf16),
        pltpu.VMEM((3, rows, width), bf16),
        *sem_pair(7 * len(orders)),
    ]


def call(kernel, number, outputs, scratch, *operands):
    return pl.pallas_call(
        kernel,
        out_shape=outputs,
        in_specs=[pl.BlockSpec(memory_space=pltpu.VMEM)] * len(operands),
        out_specs=jax.tree.map(lambda _: pl.BlockSpec(memory_space=pltpu.VMEM), outputs),
        scratch_shapes=scratch,
        compiler_params=pltpu.CompilerParams(
            collective_id=number, has_side_effects=True, vmem_limit_bytes=vmem_limit
        ),
    )(*operands)


def start_all(copies):
    for copy in copies:
        copy.start()
    return copies


def wait_all(copies):
    for copy in copies:
        copy.wait()


def spread_start(sources, targets, sems, number=0):
    me = square_place(0)
    copies = []
    for source, (target, at) in zip(sources, targets):
        size = source.shape[1] // 4
        into = target.at[me, :, pl.ds(at, size)]

        def piece(place, source=source, size=size):
            return source.at[:, pl.ds(pl.multiple_of(place * size, size), size)]

        for step in (3, 1, 2):
            away = piece(square_place(step))
            copies.append(copy_to(square_id(step), away, into, sems, number + step))
        copies.append(pltpu.make_async_copy(piece(me), into, sems[0].at[number]))
        number += 4
    return start_all(copies)


def collect_start(sources, targets, sems):
    me = square_place(0)
    copies = []
    for number, ((source, at), target) in enumerate(zip(sources, targets)):
        size = target.shape[1] // 4
        into = target.at[:, pl.ds(pl.multiple_of(me * size, size), size)]
        for step in (3, 1, 2):
            away = source.at[square_place(step), :, pl.ds(at, size)]
            copies.append(copy_to(square_id(step), away, into, sems, number * 4 + step))
        copies.append(
            pltpu.make_async_copy(source.at[me, :, pl.ds(at, size)], into, sems[0].at[number * 4])
        )
    return start_all(copies)


def enter_kernel(query, key, value, output, segments, slabs, segments_all, *sems):
    greet(square)
    size, other = query.shape[1] // 4, key.shape[1] // 4
    targets = [(slabs, at) for at in (0, size, size + other, size + 2 * other)]
    copies = spread_start((query, key, value, output), targets, sems[:2])
    segments_all[0] = segments[...]
    copies += start_all(
        [
            copy_to(
                square_id(step),
                segments,
                segments_all.at[step // 2 + step % 2 * 2],
                sems[2:],
                step,
            )
            for step in (1, 2, 3)
        ]
    )
    wait_all(copies)


def tokens_kernel(tokens, gate, up, down, inputs_all, gate_up_slabs, down_slabs, *sems):
    greet(square + [("y", 1)])

    def norm(row):
        normed, _ = normalize(tokens[row].astype(f32))
        inputs_all[0, row] = normed.astype(bf16)

    over_rows(tokens.shape[0], norm)
    hidden = gate.shape[1] // 4
    targets = ((gate_up_slabs, 0), (gate_up_slabs, hidden), (down_slabs, 0))
    gather = gather_start(inputs_all, sems[:2])
    copies = spread_start((gate, up, down), targets, sems[2:])
    gather_finish(*gather)
    wait_all(copies)


def grads_kernel(grads, grads_all, *sems):
    greet(layer)
    grads_all[0] = grads[...]
    gather_blocks(grads_all, sems)


def turn(value, cosine, sine):
    return value * cosine + pltpu.roll(value, value.shape[1] // 2, 1) * sine


def allowed_of(start):
    rows = lax.broadcasted_iota(jnp.int32, start.shape, 0)
    columns = lax.broadcasted_iota(jnp.int32, start.shape, 1)
    return (columns >= start) & (columns <= rows)


def probabilities(queries, keys, allowed):
    scores = dot_nt(queries, keys) * queries.shape[1] ** (-0.5)
    scores = jnp.where(allowed, scores, -1e30)
    powers = jnp.exp(scores - jnp.max(scores, axis=1, keepdims=True))
    return powers / jnp.sum(powers, axis=1, keepdims=True)


def head_columns(heads, groups, size):
    query = [pl.ds(h * size, size) for h in range(heads)]
    key = [pl.ds((heads + g) * size, size) for g in range(groups)]
    value = [pl.ds((heads + groups + g) * size, size) for g in range(groups)]
    return query, key, value


def middle_kernel(counts, qkv, cosine, sine, start, gains, output, tokens, attended,
                  residual, inputs_all, partial, *scratch):
    greet(layer)
    heads, groups, size = counts
    rows = tokens.shape[0]
    query, key, value = head_columns(heads, groups, size)
    total = Scatter(partial, scratch[:6])
    for i in block_order:
        row = pl.ds(i * rows, rows)
        cos, sin = cosine[row], sine[row]
        allowed = allowed_of(start[row])
        for g in range(groups):
            keys = turn(normalize(qkv[row, key[g]])[0] * gains[1:2], cos, sin).astype(bf16)
            values = qkv[row, value[g]].astype(bf16)
            for h in range(g * (heads // groups), (g + 1) * (heads // groups)):
                queries = normalize(qkv[row, query[h]])[0] * gains[0:1]
                queries = turn(queries, cos, sin).astype(bf16)
                probs = probabilities(queries, keys, allowed)
                attended[row, query[h]] = dot(probs.astype(bf16), values).astype(bf16)
        product = output[:, pl.ds(output.shape[1] - heads * size, heads * size)]
        partial[i] = dot_nt(attended[row], product).astype(bf16)
        total.ready(i)
    total.run()

    def norm(row):
        value = total.row(row) + tokens[row].astype(f32)
        residual[row] = value
        inputs_all[0, row] = normalize(value)[0].astype(bf16)

    over_rows(rows, norm)
    gather_blocks(inputs_all, scratch[6:8])


def back_kernel(partial, residual, grads, d_residual, low_all, *scratch):
    greet(layer)
    total = Scatter(partial, scratch[:6])
    for i in block_order:
        total.ready(i)
    total.run()

    def norm(row):
        normed, inverse = normalize(residual[row])
        value = grads[row].astype(f32) + norm_back(total.row(row), normed, inverse)
        d_residual[row] = value
        low_all[0, row] = value.astype(bf16)

    over_rows(residual.shape[0], norm)
    gather_blocks(low_all, scratch[6:8])


def share_start(own, both, sems):
    mine = lax.axis_index("y")
    return start_all(
        [
            copy_to(neighbour("y"), own, both.at[mine], sems, 0),
            pltpu.make_async_copy(own, both.at[mine], sems[0].at[1]),
        ]
    )


def heads_kernel(counts, rows, qkv, cosine, sine, start, gains, d_attended, d_qkv, gain_sums):
    heads, groups, size = counts
    scale = size ** (-0.5)
    query, key, value = head_columns(heads, groups, size)
    query_sum = jnp.zeros((1, size), f32)
    key_sum = jnp.zeros((1, size), f32)
    for i in range(8):
        row = pl.ds(i * rows, rows)
        cos, sin = cosine[row], sine[row]
        allowed = allowed_of(start[row])
        for g in range(groups):
            key_hat, key_inverse = normalize(qkv[row, key[g]])
            keys = turn(key_hat * gains[1:2], cos, sin).astype(bf16)
            values = qkv[row, value[g]].astype(bf16)
            d_keys = d_values = 0.0
            for h in range(g * (heads // groups), (g + 1) * (heads // groups)):
                query_hat, query_inverse = normalize(qkv[row, query[h]])
                queries = turn(query_hat * gains[0:1], cos, sin).astype(bf16)
                probs = probabilities(queries, keys, allowed)
                upstream = d_attended[row, query[h]]
                d_values = d_values + dot_tn(probs.astype(bf16), upstream)
                d_probs = dot_nt(upstream, values)
                inner = jnp.sum(d_probs * probs, axis=1, keepdims=True)
                d_scores = (probs * (d_probs - inner)).astype(bf16)
                d_keys = d_keys + dot_tn(d_scores, queries)
                d_query = turn(dot(d_scores, keys) * scale, cos, -sin)
                query_sum = query_sum + jnp.sum(d_query * query_hat, axis=0, keepdims=True)
                d_qkv[row, query[h]] = norm_back(
                    d_query * gains[0:1], query_hat, query_inverse
                ).astype(bf16)
            d_key = turn(d_keys * scale, cos, -sin)
            key_sum = key_sum + jnp.sum(d_key * key_hat, axis=0, keepdims=True)
            d_qkv[row, key[g]] = norm_back(d_key * gains[1:2], key_hat, key_inverse).astype(bf16)
            d_qkv[row, value[g]] = d_values.astype(bf16)
    gain_sums[0:1] = query_sum
    gain_sums[1:2] = key_sum


def leave_kernel(depth, partial, mixed_partial, tokens, residual, d_residual,
                 gain_sums, grad_tokens, mixed_own, gain_totals, token_grads, *scratch):
    stages = layer + [("z", 1 << n) for n in range(depth.bit_length() - 1)]
    greet(stages)
    total = Scatter(partial, scratch[:6])
    other = Scatter(mixed_partial, scratch[6:12])
    for scatter in (total, other):
        for i in block_order:
            scatter.ready(i)
    held, arrived, sems = scratch[12], scratch[13], scratch[14:16]
    held[0] = gain_sums[...]
    ticks = total.steps()
    for n, axis in enumerate(stages):
        copy = copy_to(neighbour(*axis), held.at[n], arrived.at[n], sems, n)
        copy.start()
        next(ticks, None)
        copy.wait()
        held[n + 1] = held[n] + arrived[n]
    gain_totals[...] = held[len(stages)]
    other_ticks = other.steps()
    for _ in ticks:
        next(other_ticks, None)

    def norm(row):
        normed, inverse = normalize(tokens[row].astype(f32))
        value = d_residual[row] + norm_back(total.row(row), normed, inverse)
        token_grads[row] = value.astype(bf16)

    over_rows(tokens.shape[0], norm)
    shared = share_start(token_grads, grad_tokens, scratch[16:18])
    for _ in other_ticks:
        pass

    def add(row):
        mixed_own[row] = (residual[row] + other.row(row)).astype(bf16)

    over_rows(tokens.shape[0], add)
    wait_all(shared)


def gate_up_kernel(slabs, down_slabs, mixed_own, grad_gate, grad_up, grad_down, mixed, *sems):
    greet(square + [("y", 1)])
    shared = share_start(mixed_own, mixed, sems[2:])
    sources = ((slabs, 0), (slabs, grad_gate.shape[1] // 4), (down_slabs, 0))
    wait_all(collect_start(sources, (grad_gate, grad_up, grad_down), sems[:2]))
    wait_all(shared)


def collect_kernel(slabs, grad_query, grad_key, grad_value, grad_output, *sems):
    greet(square)
    size, other = grad_query.shape[1] // 4, grad_key.shape[1] // 4
    sources = ((slabs, 0), (slabs, size), (slabs, size + other), (slabs, size + 2 * other))
    targets = (grad_query, grad_key, grad_value, grad_output)
    wait_all(collect_start(sources, targets, sems))


def tables(segments, size):
    rows = segments.shape[1]
    index_row = jnp.arange(rows)
    same_seg = segments[:, :, None] == segments[:, None, :]
    earlier = index_row[:, None] > index_row[None, :]
    position = jnp.sum(jnp.where(same_seg & earlier, 1, 0), axis=-1)
    frequency = rope_base ** (-2.0 * jnp.arange(size // 2).astype(f32) / size)
    angles = (position.astype(f32)[:, :, None] * frequency).reshape(-1, size // 2)
    cosine, sine = jnp.cos(angles), jnp.sin(angles)
    first = (index_row - position).reshape(-1, 1)
    return (
        jnp.concatenate([cosine, cosine], axis=1),
        jnp.concatenate([-sine, sine], axis=1),
        jnp.broadcast_to(first, (first.shape[0], rows)).astype(jnp.int32),
    )


def swap(values, axis):
    return lax.ppermute(values, axis, [(0, 1), (1, 0)])


def fetch(spread):
    columns = spread.shape[2]
    return lax.all_gather(spread.reshape(-1, columns), "z", axis=0, tiled=True)


def give_back(grads):
    summed_rows = lax.psum_scatter(grads, "z", scatter_dimension=0, tiled=True)
    return summed_rows.reshape(4, -1, grads.shape[1])


def on_device(depth, tokens, grad_out, segments, attention_gain, query_weight, key_weight,
              value_weight, output_weight, query_gain, key_gain, feedforward_gain, gate_weight,
              up_weight, down_weight):
    size = query_gain.shape[0]
    blocks, rows = segments.shape
    width = tokens.shape[1]
    rows_here = attention_gain.shape[0]
    heads = query_weight.shape[1] // size // 4
    groups = key_weight.shape[1] // size // 4
    counts = (heads, groups, size)
    mine = lax.axis_index("y")
    gain_one, gain_two = attention_gain[:, None], feedforward_gain[:, None]

    def array(dtype, *dims):
        return jax.ShapeDtypeStruct(dims, dtype)

    def scaled(weight, gain):
        return (weight.astype(f32) * gain).astype(bf16)

    def own(values):
        return lax.dynamic_index_in_dim(
            values.reshape(2, -1, values.shape[-1]), mine, 0, keepdims=False
        )

    token_own, grad_own = own(tokens), own(grad_out)
    block_rows = token_own.shape[0]
    block = array(f32, block_rows, width)
    both = array(bf16, 2, block_rows, width)
    everyone = array(bf16, 8, block_rows, width)
    qkv_size = (heads + 2 * groups) * size
    output_size = heads * size
    hidden_size = gate_weight.shape[1] // 4

    def scatter_shapes():
        return scatter_scratch(block_rows, width)

    pairs = segments.reshape(2, -1, rows)
    pairs = jnp.where(mine == 0, pairs, pairs[::-1]).reshape(blocks, rows)
    attention_slabs, segments_all = call(
        enter_kernel,
        1,
        (array(bf16, 4, rows_here, qkv_size + output_size), array(jnp.int32, 4, blocks, rows)),
        sem_pair(16) + sem_pair(4),
        *(scaled(w, gain_one) for w in (query_weight, key_weight, value_weight)),
        output_weight.T,
        pairs,
    )
    attention_all = fetch(attention_slabs)
    qkv_weight = attention_all[:, :qkv_size]
    token_own, _ = lax.optimization_barrier((token_own, segments_all))
    input_one, gate_up_slabs, down_slabs = call(
        tokens_kernel,
        2,
        (
            everyone,
            array(bf16, 4, rows_here, 2 * hidden_size),
            array(bf16, 4, rows_here, hidden_size),
        ),
        sem_pair(14) + sem_pair(12),
        token_own,
        scaled(gate_weight, gain_two),
        scaled(up_weight, gain_two),
        down_weight.T,
    )
    input_one = input_one.reshape(-1, width)
    gate_up_all = fetch(gate_up_slabs)
    down_all = fetch(down_slabs)
    cosine, sine, start = tables(segments_all.reshape(-1, rows), size)
    gains = jnp.stack([query_gain, key_gain])

    qkv = dot(input_one, qkv_weight)
    attended, residual, input_two = call(
        functools.partial(middle_kernel, counts),
        3,
        (array(bf16, 8 * block_rows, output_size), block, everyone),
        [pltpu.VMEM((8, block_rows, width), bf16)] + scatter_shapes() + sem_pair(14),
        qkv,
        cosine,
        sine,
        start,
        gains,
        attention_all,
        token_own,
    )
    input_two = input_two.reshape(-1, width)
    grad_own, _ = lax.optimization_barrier((grad_own, residual))
    grads_all = call(grads_kernel, 4, everyone, sem_pair(14), grad_own).reshape(-1, width)

    gate_up = dot(input_two, gate_up_all)
    gate_pre, up_pre = gate_up[:, :hidden_size], gate_up[:, hidden_size:]
    sigma = jax.nn.sigmoid(gate_pre)
    hidden = (gate_pre * sigma * up_pre).astype(bf16)
    grad_down = dot_tn(grads_all, hidden).astype(bf16)
    _, hidden, gate_pre, up_pre, down_all = lax.optimization_barrier(
        (grad_down, hidden, gate_pre, up_pre, down_all)
    )
    sigma = jax.nn.sigmoid(gate_pre)
    grad_down = give_back(grad_down)
    d_hidden = dot(grads_all, down_all)
    d_gate = (d_hidden * up_pre * sigma * (1.0 + gate_pre * (1.0 - sigma))).astype(bf16)
    d_up = (d_hidden * gate_pre * sigma).astype(bf16)
    d_gate_up = jnp.concatenate([d_gate, d_up], axis=1)
    grad_gate_up = dot_tn(input_two, d_gate_up).astype(bf16)
    partial = dot_nt(d_gate_up, gate_up_all).astype(bf16).reshape(8, -1, width)
    grad_gate_up, partial = lax.optimization_barrier((grad_gate_up, partial))
    d_residual, d_residual_low = call(
        back_kernel,
        5,
        (block, everyone),
        scatter_shapes() + sem_pair(14),
        partial,
        residual,
        grad_own,
    )
    d_residual_low = d_residual_low.reshape(-1, width)
    grad_gate_up = give_back(grad_gate_up)

    grad_output = dot_tn(d_residual_low, attended).astype(bf16)
    d_attended = dot(d_residual_low, attention_all[:, qkv_size:]).astype(bf16)
    d_qkv, gain_sums = pl.pallas_call(
        functools.partial(heads_kernel, counts, block_rows),
        out_shape=(array(bf16, 8 * block_rows, qkv_size), array(f32, 2, size)),
        in_specs=[pl.BlockSpec(memory_space=pltpu.VMEM)] * 6,
        out_specs=(pl.BlockSpec(memory_space=pltpu.VMEM),) * 2,
        compiler_params=pltpu.CompilerParams(vmem_limit_bytes=vmem_limit),
        name="heads",
    )(qkv, cosine, sine, start, gains, d_attended)
    grad_attention = jnp.concatenate(
        [dot_tn(input_one, d_qkv).astype(bf16), grad_output], axis=1
    )
    late, d_last, grad_attention = lax.optimization_barrier((hidden, d_qkv, grad_attention))
    partial = dot_nt(d_last, qkv_weight).astype(bf16).reshape(8, -1, width)
    mixed_partial = dot_nt(late, down_all).astype(bf16).reshape(8, -1, width)
    grad_attention = give_back(grad_attention)
    stages = 3 + depth.bit_length() - 1
    grad_tokens, mixed_own, head_gains = call(
        functools.partial(leave_kernel, depth),
        7,
        (
            both,
            array(bf16, block_rows, width),
            array(f32, 2, size),
        ),
        [pltpu.VMEM((block_rows, width), bf16)]
        + scatter_shapes()
        + scatter_shapes()
        + [pltpu.VMEM((stages + 1, 2, size), f32), pltpu.VMEM((stages, 2, size), f32)]
        + sem_pair(stages)
        + sem_pair(2),
        partial,
        mixed_partial,
        token_own,
        residual,
        d_residual,
        gain_sums,
    )
    raw_gate, raw_up, raw_down, mixed = call(
        gate_up_kernel,
        8,
        (*(array(bf16, rows_here, 4 * hidden_size) for _ in range(3)), both),
        sem_pair(12) + sem_pair(2),
        grad_gate_up,
        grad_down,
        mixed_own,
    )
    grad_attention, _ = lax.optimization_barrier((grad_attention, mixed))
    raw_query, raw_key, raw_value, raw_output = call(
        collect_kernel,
        9,
        (
            array(bf16, *query_weight.shape),
            array(bf16, *key_weight.shape),
            array(bf16, *value_weight.shape),
            array(bf16, rows_here, 4 * output_size),
        ),
        sem_pair(16),
        grad_attention,
    )

    def finish(raw, weights, gain):
        raw = [g.astype(f32) for g in raw]
        sums = sum(jnp.sum(w.astype(f32) * g, axis=1) for w, g in zip(weights, raw))
        sums = sums.reshape(1, rows_here)
        return [g * gain for g in raw], (sums + swap(sums, "y"))[0]

    (grad_query, grad_key, grad_value), grad_one = finish(
        (raw_query, raw_key, raw_value), (query_weight, key_weight, value_weight), gain_one
    )
    (grad_gate, grad_up), grad_two = finish((raw_gate, raw_up), (gate_weight, up_weight), gain_two)
    return (
        mixed.reshape(-1, width),
        grad_tokens.reshape(-1, width).astype(f32),
        grad_one,
        grad_query,
        grad_key,
        grad_value,
        raw_output.T.astype(f32),
        head_gains[0],
        head_gains[1],
        grad_two,
        grad_gate,
        grad_up,
        raw_down.T.astype(f32),
    )


def solution(mesh):
    depth = mesh.shape["fsdp"] // 4
    fine = Mesh(
        mesh.devices.reshape(depth, 2, 2, mesh.shape["tensor"]), ("z", "x", "core", "y")
    )
    fsdp = ("z", "x", "core")
    whole, both, turned, flat = P(fsdp, None), P(fsdp, "y"), P("y", fsdp), P(fsdp)

    def step(*arrays):
        return on_device(depth, *arrays)

    return jax.shard_map(
        step,
        mesh=fine,
        in_specs=(
            whole, whole, whole, flat, both, both, both, turned, P(), P(), flat, both, both, turned
        ),
        out_specs=(
            whole, whole, flat, both, both, both, turned, P(), P(), flat, both, both, turned
        ),
        check_vma=False,
    )
```

profile of v0, /device:TPU:0, one launch (start us, length us, event | category | flops | bytes accessed | tf_op | source)
XLA Modules:
  0.0 661.8 jit_solution(2466930496230899615)
XLA Ops:
  12.0 14.1 %shard_map.237 = (bf16[4,128,768]{2,1,0:T(8,128)(2,1)}, s32[4,2,128]{2,1,0:T(2,128)S(1)}) custom-call(bf16[128,1024]{1,0:T(8,128)(2,1)S(1)} %fusion.8.query, bf16[128,512]{1,0:T(8,128)(2,1)S(1)} %get-tuple-element.138.key, bf16[128,512]{1,0:T(8,128)(2,1)S(1)} %get-tuple-element.137.value, bf16[128,1024]{1,0:T(8,128)(2,1)S(1)} %bitcast.76, ...), custom_call_target="tpu_custom_call" | custom-call | tf_op jit(solution)/shard_map/pallas_call | solution.py:224
  29.3 48.7 %shard_map.238 = (bf16[8,128,2048]{2,1,0:T(8,128)(2,1)S(1)}, bf16[4,128,1536]{2,1,0:T(8,128)(2,1)S(1)}, bf16[4,128,768]{2,1,0:T(8,128)(2,1)}) custom-call(bf16[128,2048]{1,0:T(8,128)(2,1)S(1)} %dynamic-slice_bitcast_fusion.1.tokens, bf16[128,3072]{1,0:T(8,128)(2,1)S(1)} %get-tuple-element.136.gate, bf16[128,3072]{1,0:T(8,128)(2,1)S(1)} %get-tuple-element.135.up, ...), custom_call_target="tpu_custom_call" | custom-call | tf_op jit(solution)/shard_map/pallas_call | solution.py:224
  79.2 1.9 copy-done.19
  86.3 4.2 all-gather.4.cloned.1.call-done.output
  90.5 5.3 fusion.1.qkv
  96.1 50.5 %shard_map.239 = (bf16[1024,256]{1,0:T(8,128)(2,1)S(1)}, f32[128,2048]{1,0:T(8,128)S(1)}, bf16[8,128,2048]{2,1,0:T(8,128)(2,1)S(1)}) custom-call(f32[1024,512]{1,0:T(8,128)S(1)} %fusion.1.qkv, f32[1024,128]{1,0:T(8,128)S(1)} %get-tuple-element.139.cosine, f32[1024,128]{1,0:T(8,128)S(1)} %copy-done.2, s32[1024,128]{1,0:T(8,128)S(1)} %broadcast_in_dim.12.start, ...), custom_call_target="tpu_custom_call" | custom-call | tf_op jit(solution)/shard_map/pallas_call | solution.py:224
  148.5 2.1 copy-done.21
  150.5 22.0 %shard_map.240 = bf16[8,128,2048]{2,1,0:T(8,128)(2,1)S(1)} custom-call(bf16[128,2048]{1,0:T(8,128)(2,1)S(1)} %copy-done.6), custom_call_target="tpu_custom_call" | custom-call | tf_op jit(solution)/shard_map/pallas_call | solution.py:224
  172.6 2.0 copy-done.8
  174.6 32.1 %all-gather.6.cloned.1.call-done = bf16[2048,1536]{1,0:T(8,128)(2,1)} async-done(((bf16[512,1536]{1,0:T(8,128)(2,1)}), bf16[2048,1536]{1,0:T(8,128)(2,1)}) %all-gather.6.cloned.1.call-update) | async-done | bytes 6291472 | tf_op jit(solution)/shard_map/all_gather | solution.py:524
  206.7 10.0 %fusion.18 = f32[1024,1536]{1,0:T(8,128)S(1)} fusion(bf16[1024,2048]{1,0:T(8,128)(2,1)} %bitcast.81, bf16[2048,1536]{1,0:T(8,128)(2,1)} %all-gather.6.cloned.1.call-done), kind=kOutput, calls=%fused_computation.69 | convolution fusion | flops 6442450944 | bytes 16777216 | tf_op jit(solution)/shard_map/dot_general | solution.py:35
  216.7 3.7 fusion.17
  221.6 5.0 convolution_convert_fusion.4
  226.6 43.4 %all-gather.8.cloned.1.call-done = bf16[2048,768]{1,0:T(8,128)(2,1)} async-done(((bf16[512,768]{1,0:T(8,128)(2,1)}), bf16[2048,768]{1,0:T(8,128)(2,1)}) %all-gather.8.cloned.1.call-update) | async-done | bytes 3145744 | tf_op jit(solution)/shard_map/all_gather | solution.py:524
  269.9 9.2 %multiply_convert_fusion.1 = (bf16[1024,768]{1,0:T(8,128)(2,1)S(1)}, bf16[1024,768]{1,0:T(8,128)(2,1)S(1)}) fusion(f32[1024,768]{1,0:T(8,128)} %get-tuple-element.59, f32[1024,768]{1,0:T(8,128)} %get-tuple-element.58, bf16[1024,2048]{1,0:T(8,128)(2,1)} %bitcast.66, bf16[2048,768]{1,0:T(8,128)(2,1)} %all-gather.8.cloned.1.call-done), kind=kOutput, calls=%fused_computation.8 | convolution fusion | flops 3231449088 | bytes 16777216 | tf_op jit(solution)/shard_map/dot_general | solution.py:35
  280.8 9.4 %convolution_convert_fusion = bf16[2048,1536]{1,0:T(8,128)(2,1)} fusion(bf16[1024,2048]{1,0:T(8,128)(2,1)S(1)} %bitcast.82, bf16[1024,768]{1,0:T(8,128)(2,1)S(1)} %get-tuple-element.110, bf16[1024,768]{1,0:T(8,128)(2,1)S(1)} %get-tuple-element.109), kind=kOutput, calls=%fused_computation | convolution fusion | flops 6451888128 | bytes 13631488 | tf_op jit(solution)/shard_map/dot_general | solution.py:39
  290.2 9.9 %convolution_convert_fusion.1 = bf16[1024,2048]{1,0:T(8,128)(2,1)S(1)} fusion(bf16[2048,1536]{1,0:T(8,128)(2,1)} %all-gather.6.cloned.1.call-done, bf16[1024,768]{1,0:T(8,128)(2,1)} %copy-done.42, bf16[1024,768]{1,0:T(8,128)(2,1)} %copy-done.41), kind=kOutput, calls=%fused_computation.1 | convolution fusion | flops 6450839552 | bytes 13631488 | tf_op jit(solution)/shard_map/dot_general | solution.py:43
  300.1 45.4 %shard_map.241 = (f32[128,2048]{1,0:T(8,128)S(1)}, bf16[8,128,2048]{2,1,0:T(8,128)(2,1)S(1)}) custom-call(bf16[8,128,2048]{2,1,0:T(8,128)(2,1)S(1)} %bitcast.70, f32[128,2048]{1,0:T(8,128)S(1)} %copy-done.11, bf16[128,2048]{1,0:T(8,128)(2,1)S(1)} %copy-done.7), custom_call_target="tpu_custom_call" | custom-call | tf_op jit(solution)/shard_map/pallas_call | solution.py:224
  346.9 2.6 convolution_convert_fusion.7.d_attended
  349.5 7.7 %heads.1 = (bf16[1024,512]{1,0:T(8,128)(2,1)S(1)}, f32[2,128]{1,0:T(2,128)S(1)}) custom-call(f32[1024,512]{1,0:T(8,128)S(1)} %fusion.1.qkv, f32[1024,128]{1,0:T(8,128)S(1)} %get-tuple-element.139.cosine, f32[1024,128]{1,0:T(8,128)S(1)} %copy-done.3, s32[1024,128]{1,0:T(8,128)S(1)} %copy-done.5, f32[2,128]{1,0:T(2,128)S(1)} %pad_maximum_fusion.6.gains, ...), custom_call_target="tpu_custom_call" | custom-call | tf_op jit(solution)/shard_map/heads/pallas_call | solution.py:651
  357.2 2.5 convolution_convert_fusion.5
  359.7 2.0 pad_maximum_fusion.1
  363.5 4.1 convolution_convert_fusion.2
  367.7 3.7 convolution_convert_fusion.3
  371.4 54.5 %shard_map.242 = (bf16[2,128,2048]{2,1,0:T(8,128)(2,1)S(1)}, bf16[128,2048]{1,0:T(8,128)(2,1)S(1)}, f32[2,128]{1,0:T(2,128)S(1)}) custom-call(bf16[8,128,2048]{2,1,0:T(8,128)(2,1)S(1)} %bitcast.68, bf16[8,128,2048]{2,1,0:T(8,128)(2,1)S(1)} %bitcast.69, bf16[128,2048]{1,0:T(8,128)(2,1)S(1)} %dynamic-slice_bitcast_fusion.1.tokens, f32[128,2048]{1,0:T(8,128)S(1)} %copy-done.12, ...), custom_call_target="tpu_custom_call" | custom-call | tf_op jit(solution)/shard_map/pallas_call | solution.py:224
  429.6 52.8 %reduce-scatter.6.cloned.1.call-done = bf16[512,768]{1,0:T(8,128)(2,1)} async-done(((bf16[2048,768]{1,0:T(8,128)(2,1)}), bf16[512,768]{1,0:T(8,128)(2,1)}) %reduce-scatter.6.cloned.1.call-update) | async-done | bytes 786448 | tf_op jit(solution)/shard_map/reduce_scatter | solution.py:528
  482.4 112.9 %reduce-scatter.4.cloned.1.call-done = bf16[512,1536]{1,0:T(8,128)(2,1)} async-done(((bf16[2048,1536]{1,0:T(8,128)(2,1)}), bf16[512,1536]{1,0:T(8,128)(2,1)}) %reduce-scatter.4.cloned.1.call-update) | async-done | bytes 1572880 | tf_op jit(solution)/shard_map/reduce_scatter | solution.py:528
  597.8 28.9 %shard_map.243 = (bf16[128,3072]{1,0:T(8,128)(2,1)S(1)}, bf16[128,3072]{1,0:T(8,128)(2,1)S(1)}, bf16[128,3072]{1,0:T(8,128)(2,1)S(1)}, bf16[2,128,2048]{2,1,0:T(8,128)(2,1)S(1)}) custom-call(bf16[4,128,1536]{2,1,0:T(8,128)(2,1)S(1)} %bitcast.74, bf16[4,128,768]{2,1,0:T(8,128)(2,1)S(1)} %bitcast.77, bf16[128,2048]{1,0:T(8,128)(2,1)S(1)} %get-tuple-element.70.mixed_own), custom_call_target="tpu_custom_call" | custom-call | tf_op jit(solution)/shard_map/pallas_call | solution.py:224
  626.7 11.8 %shard_map.244 = (bf16[128,1024]{1,0:T(8,128)(2,1)S(1)}, bf16[128,512]{1,0:T(8,128)(2,1)S(1)}, bf16[128,512]{1,0:T(8,128)(2,1)S(1)}, bf16[128,1024]{1,0:T(8,128)(2,1)S(1)}) custom-call(bf16[4,128,768]{2,1,0:T(8,128)(2,1)S(1)} %bitcast.71), custom_call_target="tpu_custom_call" | custom-call | tf_op jit(solution)/shard_map/pallas_call | solution.py:224
  642.9 2.5 convert_multiply_fusion
  646.4 3.0 copy.40
  650.8 2.2 collective-permute-done.1
  (130 shorter events, 36.5 us)
Async XLA Ops:
  7.2 19.1 %copy-start = (bf16[256,2048]{1,0:T(8,128)(2,1)S(1)}, bf16[256,2048]{1,0:T(8,128)(2,1)}, u32[]{:S(2)}) copy-start(bf16[256,2048]{1,0:T(8,128)(2,1)} %param.14) | copy-start | bytes 3145732
  7.2 20.5 %copy-start.27 = (bf16[128,3072]{1,0:T(8,128)(2,1)S(1)}, bf16[128,3072]{1,0:T(8,128)(2,1)}, u32[]{:S(2)}) copy-start(bf16[128,3072]{1,0:T(8,128)(2,1)} %param.26) | copy-start | bytes 2359300
  7.2 20.5 %copy-start.37 = (f32[128]{0:T(128)S(1)}, f32[128]{0:T(128)}, u32[]{:S(2)}) copy-start(f32[128]{0:T(128)} %param.24) | copy-start | bytes 1540
  7.2 83.3 %all-gather.4.cloned.1.call-start = ((), (), s32[]{:S(2)}) async-start(), calls=%async_computation.3 | async-start | bytes 3932160 | tf_op jit(solution)/shard_map/all_gather | solution.py:524
  26.2 180.5 %all-gather.6.cloned.1.call-start = ((), (), s32[]{:S(2)}) async-start(), calls=%async_computation.4 | async-start | bytes 7864320 | tf_op jit(solution)/shard_map/all_gather | solution.py:524
  29.3 53.1 %copy-start.38 = (f32[128]{0:T(128)S(1)}, f32[128]{0:T(128)}, u32[]{:S(2)}) copy-start(f32[128]{0:T(128)} %param.23) | copy-start | bytes 1540
  29.3 53.1 %copy-start.39 = (f32[128]{0:T(128)S(1)}, f32[128]{0:T(128)}, u32[]{:S(2)}) copy-start(f32[128]{0:T(128)} %param.22) | copy-start | bytes 1540
  81.2 4.3 copy-start.35
  81.2 188.7 %all-gather.8.cloned.1.call-start = ((), (), s32[]{:S(2)}) async-start(), calls=%async_computation.5 | async-start | bytes 3932160 | tf_op jit(solution)/shard_map/all_gather | solution.py:524
  81.9 346.2 %reduce-scatter.8.cloned.1.call-start = ((), (), s32[]{:S(2)}) async-start(), calls=%async_computation.8 | async-start | bytes 3932160 | tf_op jit(solution)/shard_map/reduce_scatter | solution.py:528
  90.5 5.5 copy-start.2
  90.5 5.5 copy-start.13
  96.1 50.6 %copy-start.4 = (s32[1024,128]{1,0:T(8,128)}, s32[1024,128]{1,0:T(8,128)S(1)}, u32[]{:S(2)}) copy-start(s32[1024,128]{1,0:T(8,128)S(1)} %broadcast_in_dim.12.start) | copy-start | bytes 1572868
  96.1 54.4 %copy-start.6 = (bf16[128,2048]{1,0:T(8,128)(2,1)S(1)}, bf16[128,2048]{1,0:T(8,128)(2,1)}, u32[]{:S(2)}) copy-start(bf16[128,2048]{1,0:T(8,128)(2,1)} %dynamic-slice_bitcast_fusion.grads) | copy-start | bytes 1572868
  216.7 4.9 copy-start.9
  269.9 10.9 %copy-start.22 = (bf16[8,128,2048]{2,1,0:T(8,128)(2,1)S(1)}, bf16[8,128,2048]{2,1,0:T(8,128)(2,1)}, u32[]{:S(2)}) copy-start(bf16[8,128,2048]{2,1,0:T(8,128)(2,1)} %copy-done.21) | copy-start | bytes 12582916
  290.2 9.9 %copy-start.7 = (bf16[128,2048]{1,0:T(8,128)(2,1)S(1)}, bf16[128,2048]{1,0:T(8,128)(2,1)}, u32[]{:S(2)}) copy-start(bf16[128,2048]{1,0:T(8,128)(2,1)} %dynamic-slice_bitcast_fusion.grads) | copy-start | bytes 1572868
  290.2 9.9 %copy-start.11 = (f32[128,2048]{1,0:T(8,128)S(1)}, f32[128,2048]{1,0:T(8,128)}, u32[]{:S(2)}) copy-start(f32[128,2048]{1,0:T(8,128)} %copy-done.10) | copy-start | bytes 3145732
  300.1 45.4 %copy-start.26 = (bf16[1024,256]{1,0:T(8,128)(2,1)S(1)}, bf16[1024,256]{1,0:T(8,128)(2,1)}, u32[]{:S(2)}) copy-start(bf16[1024,256]{1,0:T(8,128)(2,1)} %copy-done.25) | copy-start | bytes 1572868
  349.5 7.7 %copy-start.20 = (bf16[8,128,2048]{2,1,0:T(8,128)(2,1)S(1)}, bf16[8,128,2048]{2,1,0:T(8,128)(2,1)}, u32[]{:S(2)}) copy-start(bf16[8,128,2048]{2,1,0:T(8,128)(2,1)} %copy-done.19) | copy-start | bytes 12582916
  361.7 120.6 %reduce-scatter.6.cloned.1.call-start = ((), (), s32[]{:S(2)}) async-start(), calls=%async_computation.7 | async-start | bytes 3932160 | tf_op jit(solution)/shard_map/reduce_scatter | solution.py:528
  362.3 232.9 %reduce-scatter.4.cloned.1.call-start = ((), (), s32[]{:S(2)}) async-start(), calls=%async_computation.6 | async-start | bytes 7864320 | tf_op jit(solution)/shard_map/reduce_scatter | solution.py:528
  363.5 4.1 copy-start.40
  428.1 210.4 %copy-start.32 = (bf16[128,1024]{1,0:T(8,128)(2,1)S(1)}, bf16[128,1024]{1,0:T(8,128)(2,1)}, u32[]{:S(2)}) copy-start(bf16[128,1024]{1,0:T(8,128)(2,1)} %param.18) | copy-start | bytes 786436
  428.1 210.4 %copy-start.36 = (f32[128]{0:T(128)S(1)}, f32[128]{0:T(128)}, u32[]{:S(2)}) copy-start(f32[128]{0:T(128)} %param.17) | copy-start | bytes 1540
  428.1 211.3 %copy-start.33 = (bf16[128,512]{1,0:T(8,128)(2,1)S(1)}, bf16[128,512]{1,0:T(8,128)(2,1)}, u32[]{:S(2)}) copy-start(bf16[128,512]{1,0:T(8,128)(2,1)} %param.20) | copy-start | bytes 393220
  428.1 211.3 %copy-start.34 = (bf16[128,512]{1,0:T(8,128)(2,1)S(1)}, bf16[128,512]{1,0:T(8,128)(2,1)}, u32[]{:S(2)}) copy-start(bf16[128,512]{1,0:T(8,128)(2,1)} %param.19) | copy-start | bytes 393220
  626.7 16.2 %copy-start.28 = (bf16[128,3072]{1,0:T(8,128)(2,1)S(1)}, bf16[128,3072]{1,0:T(8,128)(2,1)}, u32[]{:S(2)}) copy-start(bf16[128,3072]{1,0:T(8,128)(2,1)} %param.26) | copy-start | bytes 2359300
  626.7 16.2 %copy-start.29 = (bf16[128,3072]{1,0:T(8,128)(2,1)S(1)}, bf16[128,3072]{1,0:T(8,128)(2,1)}, u32[]{:S(2)}) copy-start(bf16[128,3072]{1,0:T(8,128)(2,1)} %param.25) | copy-start | bytes 2359300
  640.3 10.0 %collective-permute-start = (f32[1,128]{1,0:T(1,128)S(1)}, f32[1,128]{1,0:T(1,128)S(1)}, u32[]{:S(2)}, u32[]{:S(2)}) collective-permute-start(f32[1,128]{1,0:T(1,128)S(1)} %add_bitcast_fusion.3), channel_id=1, source_target_pairs={{0,1},{1,0},{2,3},{3,2},{4,5},{5,4},{6,7},{7,6},{8,9},{9,8},{10,11... | collective-permute-start | bytes 1544 | tf_op jit(solution)/shard_map/ppermute | solution.py:519
  645.4 9.1 %copy-start.1 = (bf16[256,2048]{1,0:T(8,128)(2,1)S(1)}, bf16[256,2048]{1,0:T(8,128)(2,1)}, u32[]{:S(2)}) copy-start(bf16[256,2048]{1,0:T(8,128)(2,1)} %param.14) | copy-start | bytes 3145732
  649.4 3.6 collective-permute-start.1
  (19 other events, 37.2 us)
Sparse Core Ops, SparseCore 0:
  26.3 64.1 all-gather.3
  92.7 113.9 all-gather.5
  208.3 61.6 all-gather.7
  361.8 58.0 reduce-scatter.7
  422.0 60.2 reduce-scatter.5
  484.5 110.6 reduce-scatter.3
where the time goes:
time: 670 us; the launch traced here: 662 us
  Pallas kernels  284 us (42%)
  waiting for transfers between devices  249 us (37%)
  matrix products  62.9 us (9%)
  local copies, waits for them, and re-layouts  26.4 us (4%)
  other arithmetic  21.9 us (3%)
  between operations  15.2 us (2%)
    pallas_call x8, Pallas kernels, call(): pl.pallas_call(kernel, out_shape=outputs, in_specs=[pl.BlockSpec(memory_s...  276 us
    reduce_scatter x3, waiting for transfers between devices, give_back(): summed_rows = lax.psum_scatter(grads, 'z', scatter_dimension=0, tiled=True)  166 us
    all_gather x3, waiting for transfers between devices, fetch(): return lax.all_gather(spread.reshape(-1, columns), 'z', axis=0, tiled=True)  79.7 us
    dot_general x4, matrix products, dot(): return jnp.dot(left, right, preferred_element_type=f32)  27.1 us
    unnamed x91, local copies, waits for them, and re-layouts  22.5 us
    dot_general x4, matrix products, dot_tn(): lax.dot_general(left, right, (((0,), (0,)), ((), ())), preferred_element_...  18.2 us
    dot_general x3, matrix products, dot_nt(): lax.dot_general(left, right, (((1,), (1,)), ((), ())), preferred_element_...  17.7 us
  transfers between devices with their start and end apart: 8, of which 6 were waited for; matrix products, arithmetic and copies ran while one was open for 8% of the time, Pallas kernels for 27%

commit v1 on v0

--- a/solution.py
+++ b/solution.py
@@ -207,7 +207,17 @@
         return value + self.second[0, row].astype(f32) + self.third[0, row].astype(f32)
 
 
-block_order = (7, 6, 5, 3, 4, 2, 1, 0)
+def products(scatter, left, right, columns):
+    rows = scatter.blocks.shape[1]
+
+    def step(i, carry):
+        row = pl.ds(pl.multiple_of(i * rows, rows), rows)
+        scatter.blocks[i] = dot_nt(left[row], right[:, columns]).astype(bf16)
+        return carry
+
+    lax.fori_loop(0, 8, step, 0)
+    for i in range(4, 8):
+        scatter.ready(i)
 
 
 def scatter_scratch(rows, width):
@@ -324,10 +334,15 @@
     return value * cosine + pltpu.roll(value, value.shape[1] // 2, 1) * sine
 
 
-def allowed_of(start):
+def block_tables(start, cosine, sine):
     rows = lax.broadcasted_iota(jnp.int32, start.shape, 0)
     columns = lax.broadcasted_iota(jnp.int32, start.shape, 1)
-    return (columns >= start) & (columns <= rows)
+    pick = jnp.where(columns == rows - start, 1.0, 0.0)
+    cos, sin = (
+        jnp.dot(pick, table[...], precision=lax.Precision.HIGHEST, preferred_element_type=f32)
+        for table in (cosine, sine)
+    )
+    return (columns >= start) & (columns <= rows), cos, sin
 
 
 def probabilities(queries, keys, allowed):
@@ -351,10 +366,10 @@
     rows = tokens.shape[0]
     query, key, value = head_columns(heads, groups, size)
     total = Scatter(partial, scratch[:6])
-    for i in block_order:
-        row = pl.ds(i * rows, rows)
-        cos, sin = cosine[row], sine[row]
-        allowed = allowed_of(start[row])
+
+    def attend(i, carry):
+        row = pl.ds(pl.multiple_of(i * rows, rows), rows)
+        allowed, cos, sin = block_tables(start[row], cosine, sine)
         for g in range(groups):
             keys = turn(normalize(qkv[row, key[g]])[0] * gains[1:2], cos, sin).astype(bf16)
             values = qkv[row, value[g]].astype(bf16)
@@ -363,9 +378,10 @@
                 queries = turn(queries, cos, sin).astype(bf16)
                 probs = probabilities(queries, keys, allowed)
                 attended[row, query[h]] = dot(probs.astype(bf16), values).astype(bf16)
-        product = output[:, pl.ds(output.shape[1] - heads * size, heads * size)]
-        partial[i] = dot_nt(attended[row], product).astype(bf16)
-        total.ready(i)
+        return carry
+
+    lax.fori_loop(0, 8, attend, 0)
+    products(total, attended, output, pl.ds(output.shape[1] - heads * size, heads * size))
     total.run()
 
     def norm(row):
@@ -377,11 +393,10 @@
     gather_blocks(inputs_all, scratch[6:8])
 
 
-def back_kernel(partial, residual, grads, d_residual, low_all, *scratch):
+def back_kernel(d_gate_up, gate_up, residual, grads, d_residual, low_all, partial, *scratch):
     greet(layer)
     total = Scatter(partial, scratch[:6])
-    for i in block_order:
-        total.ready(i)
+    products(total, d_gate_up, gate_up, slice(None))
     total.run()
 
     def norm(row):
@@ -408,12 +423,11 @@
     heads, groups, size = counts
     scale = size ** (-0.5)
     query, key, value = head_columns(heads, groups, size)
-    query_sum = jnp.zeros((1, size), f32)
-    key_sum = jnp.zeros((1, size), f32)
-    for i in range(8):
-        row = pl.ds(i * rows, rows)
-        cos, sin = cosine[row], sine[row]
-        allowed = allowed_of(start[row])
+
+    def block(i, sums):
+        query_sum, key_sum = sums
+        row = pl.ds(pl.multiple_of(i * rows, rows), rows)
+        allowed, cos, sin = block_tables(start[row], cosine, sine)
         for g in range(groups):
             key_hat, key_inverse = normalize(qkv[row, key[g]])
             keys = turn(key_hat * gains[1:2], cos, sin).astype(bf16)
@@ -438,19 +452,22 @@
             key_sum = key_sum + jnp.sum(d_key * key_hat, axis=0, keepdims=True)
             d_qkv[row, key[g]] = norm_back(d_key * gains[1:2], key_hat, key_inverse).astype(bf16)
             d_qkv[row, value[g]] = d_values.astype(bf16)
+        return query_sum, key_sum
+
+    zeros = jnp.zeros((1, size), f32)
+    query_sum, key_sum = lax.fori_loop(0, 8, block, (zeros, zeros))
     gain_sums[0:1] = query_sum
     gain_sums[1:2] = key_sum
 
 
-def leave_kernel(depth, partial, mixed_partial, tokens, residual, d_residual,
-                 gain_sums, grad_tokens, mixed_own, gain_totals, token_grads, *scratch):
+def leave_kernel(depth, d_qkv, weights, hidden, down, tokens, residual, d_residual, gain_sums,
+                 grad_tokens, mixed_own, gain_totals, partial, mixed_partial, token_grads, *scratch):
     stages = layer + [("z", 1 << n) for n in range(depth.bit_length() - 1)]
     greet(stages)
     total = Scatter(partial, scratch[:6])
     other = Scatter(mixed_partial, scratch[6:12])
-    for scatter in (total, other):
-        for i in block_order:
-            scatter.ready(i)
+    products(total, d_qkv, weights, pl.ds(0, d_qkv.shape[1]))
+    products(other, hidden, down, slice(None))
     held, arrived, sems = scratch[12], scratch[13], scratch[14:16]
     held[0] = gain_sums[...]
     ticks = total.steps()
@@ -505,7 +522,7 @@
     earlier = index_row[:, None] > index_row[None, :]
     position = jnp.sum(jnp.where(same_seg & earlier, 1, 0), axis=-1)
     frequency = rope_base ** (-2.0 * jnp.arange(size // 2).astype(f32) / size)
-    angles = (position.astype(f32)[:, :, None] * frequency).reshape(-1, size // 2)
+    angles = index_row.astype(f32)[:, None] * frequency
     cosine, sine = jnp.cos(angles), jnp.sin(angles)
     first = (index_row - position).reshape(-1, 1)
     return (
@@ -632,14 +649,15 @@
     d_up = (d_hidden * gate_pre * sigma).astype(bf16)
     d_gate_up = jnp.concatenate([d_gate, d_up], axis=1)
     grad_gate_up = dot_tn(input_two, d_gate_up).astype(bf16)
-    partial = dot_nt(d_gate_up, gate_up_all).astype(bf16).reshape(8, -1, width)
-    grad_gate_up, partial = lax.optimization_barrier((grad_gate_up, partial))
+    grad_gate_up, d_gate_up = lax.optimization_barrier((grad_gate_up, d_gate_up))
+    blocks_scratch = pltpu.VMEM((8, block_rows, width), bf16)
     d_residual, d_residual_low = call(
         back_kernel,
         5,
         (block, everyone),
-        scatter_shapes() + sem_pair(14),
-        partial,
+        [blocks_scratch] + scatter_shapes() + sem_pair(14),
+        d_gate_up,
+        gate_up_all,
         residual,
         grad_own,
     )
@@ -659,9 +677,7 @@
     grad_attention = jnp.concatenate(
         [dot_tn(input_one, d_qkv).astype(bf16), grad_output], axis=1
     )
-    late, d_last, grad_attention = lax.optimization_barrier((hidden, d_qkv, grad_attention))
-    partial = dot_nt(d_last, qkv_weight).astype(bf16).reshape(8, -1, width)
-    mixed_partial = dot_nt(late, down_all).astype(bf16).reshape(8, -1, width)
+    d_qkv, grad_attention = lax.optimization_barrier((d_qkv, grad_attention))
     grad_attention = give_back(grad_attention)
     stages = 3 + depth.bit_length() - 1
     grad_tokens, mixed_own, head_gains = call(
@@ -672,14 +688,16 @@
             array(bf16, block_rows, width),
             array(f32, 2, size),
         ),
-        [pltpu.VMEM((block_rows, width), bf16)]
+        [blocks_scratch, blocks_scratch, pltpu.VMEM((block_rows, width), bf16)]
         + scatter_shapes()
         + scatter_shapes()
         + [pltpu.VMEM((stages + 1, 2, size), f32), pltpu.VMEM((stages, 2, size), f32)]
         + sem_pair(stages)
         + sem_pair(2),
-        partial,
-        mixed_partial,
+        d_qkv,
+        attention_all,
+        hidden,
+        down_all,
         token_own,
         residual,
         d_residual,

time: 670 us -> 677 us (1.010); the launches traced: 662 us -> 676 us
  Pallas kernels: 284 us -> 330 us
  matrix products: 62.9 us -> 43.8 us
  waiting for transfers between devices: 249 us -> 231 us
  local copies, waits for them, and re-layouts: 26.4 us -> 34.3 us
    pallas_call x8, Pallas kernels: 276 us -> 320 us  [call(): pl.pallas_call(kernel, out_shape=outputs, in_specs=[pl.BlockSpec(memory_s...]
    dot_general x3 -> x0, matrix products: 17.7 us -> none  [dot_nt(): lax.dot_general(left, right, (((1,), (1,)), ((), ())), preferred_element_...]
    reduce_scatter x3, waiting for transfers between devices: 166 us -> 152 us  [give_back(): summed_rows = lax.psum_scatter(grads, 'z', scatter_dimension=0, tiled=True)]
    unnamed x91 -> x101, local copies, waits for them, and re-layouts: 22.5 us -> 30.4 us
  transfers between devices with their start and end apart: 8 -> 8, of which waited for: 6 -> 6; matrix products, arithmetic and copies ran while one was open for 8% -> 6% of each run, Pallas kernels for 27% -> 29%
where the time goes in v1:
time: 677 us; the launch traced here: 676 us
  Pallas kernels  330 us (49%)
  waiting for transfers between devices  231 us (34%)
  matrix products  43.8 us (6%)
  local copies, waits for them, and re-layouts  34.3 us (5%)
  other arithmetic  20.6 us (3%)
  between operations  14.7 us (2%)
    pallas_call x8, Pallas kernels, call(): pl.pallas_call(kernel, out_shape=outputs, in_specs=[pl.BlockSpec(memory_s...  320 us
    reduce_scatter x3, waiting for transfers between devices, give_back(): summed_rows = lax.psum_scatter(grads, 'z', scatter_dimension=0, tiled=True)  152 us
    all_gather x3, waiting for transfers between devices, fetch(): return lax.all_gather(spread.reshape(-1, columns), 'z', axis=0, tiled=True)  74.4 us
    unnamed x101, local copies, waits for them, and re-layouts  30.4 us
    dot_general x4, matrix products, dot(): return jnp.dot(left, right, preferred_element_type=f32)  25.8 us
    dot_general x4, matrix products, dot_tn(): lax.dot_general(left, right, (((0,), (0,)), ((), ())), preferred_element_...  18 us
  transfers between devices with their start and end apart: 8, of which 6 were waited for; matrix products, arithmetic and copies ran while one was open for 6% of the time, Pallas kernels for 29%

profile of v1, /device:TPU:0, one launch (start us, length us, event | category | flops | bytes accessed | tf_op | source)
XLA Modules:
  0.0 676.0 jit_solution(14702903847742915944)
XLA Ops:
  12.1 14.1 %shard_map.237 = (bf16[4,128,768]{2,1,0:T(8,128)(2,1)}, s32[4,2,128]{2,1,0:T(2,128)S(1)}) custom-call(bf16[128,1024]{1,0:T(8,128)(2,1)S(1)} %fusion.7.query, bf16[128,512]{1,0:T(8,128)(2,1)S(1)} %get-tuple-element.134.key, bf16[128,512]{1,0:T(8,128)(2,1)S(1)} %get-tuple-element.133.value, bf16[128,1024]{1,0:T(8,128)(2,1)S(1)} %bitcast.63, ...), custom_call_target="tpu_custom_call" | custom-call | tf_op jit(solution)/shard_map/pallas_call | solution.py:234
  26.4 1.6 copy.35
  28.5 49.3 %shard_map.238 = (bf16[8,128,2048]{2,1,0:T(8,128)(2,1)S(1)}, bf16[4,128,1536]{2,1,0:T(8,128)(2,1)}, bf16[4,128,768]{2,1,0:T(8,128)(2,1)}) custom-call(bf16[128,2048]{1,0:T(8,128)(2,1)S(1)} %dynamic-slice_bitcast_fusion.1.tokens, bf16[128,3072]{1,0:T(8,128)(2,1)S(1)} %get-tuple-element.132.gate, bf16[128,3072]{1,0:T(8,128)(2,1)S(1)} %get-tuple-element.131.up, ...), custom_call_target="tpu_custom_call" | custom-call | tf_op jit(solution)/shard_map/pallas_call | solution.py:234
  77.8 2.0 copy-done.28
  82.3 8.3 %all-gather.4.cloned.1.call-done.output.weights = bf16[2048,768]{1,0:T(8,128)(2,1)} async-done(((bf16[512,768]{1,0:T(8,128)(2,1)}), bf16[2048,768]{1,0:T(8,128)(2,1)}) %all-gather.4.cloned.1.call-update) | async-done | bytes 3145744 | tf_op jit(solution)/shard_map/all_gather | solution.py:541
  90.6 5.3 fusion.qkv
  96.1 59.2 %shard_map.239 = (bf16[1024,256]{1,0:T(8,128)(2,1)S(1)}, f32[128,2048]{1,0:T(8,128)S(1)}, bf16[8,128,2048]{2,1,0:T(8,128)(2,1)S(1)}) custom-call(f32[1024,512]{1,0:T(8,128)S(1)} %fusion.qkv, f32[128,128]{1,0:T(8,128)S(1)} %get-tuple-element.135.cosine, f32[128,128]{1,0:T(8,128)S(1)} %get-tuple-element.136.sine, s32[1024,128]{1,0:T(8,128)S(1)} %broadcast_in_dim.12.start, ...), custom_call_target="tpu_custom_call" | custom-call | tf_op jit(solution)/shard_map/pallas_call | solution.py:234
  157.2 2.0 copy-done.30
  159.2 22.0 %shard_map.240 = bf16[8,128,2048]{2,1,0:T(8,128)(2,1)S(1)} custom-call(bf16[128,2048]{1,0:T(8,128)(2,1)S(1)} %copy-done.12), custom_call_target="tpu_custom_call" | custom-call | tf_op jit(solution)/shard_map/pallas_call | solution.py:234
  181.3 2.1 copy-done.14
  183.3 22.8 %all-gather.6.cloned.1.call-done.gate_up = bf16[2048,1536]{1,0:T(8,128)(2,1)} async-done(((bf16[512,1536]{1,0:T(8,128)(2,1)}), bf16[2048,1536]{1,0:T(8,128)(2,1)}) %all-gather.6.cloned.1.call-update) | async-done | bytes 6291472 | tf_op jit(solution)/shard_map/all_gather | solution.py:541
  206.1 10.0 %fusion.15 = f32[1024,1536]{1,0:T(8,128)S(1)} fusion(bf16[1024,2048]{1,0:T(8,128)(2,1)} %bitcast.68, bf16[2048,1536]{1,0:T(8,128)(2,1)} %all-gather.6.cloned.1.call-done.gate_up), kind=kOutput, calls=%fused_computation.63 | convolution fusion | flops 6442450944 | bytes 16777216 | tf_op jit(solution)/shard_map/dot_general | solution.py:35
  216.2 3.8 fusion.14
  220.0 4.9 convolution_convert_fusion.1
  226.0 43.4 %all-gather.8.cloned.1.call-done.down = bf16[2048,768]{1,0:T(8,128)(2,1)} async-done(((bf16[512,768]{1,0:T(8,128)(2,1)}), bf16[2048,768]{1,0:T(8,128)(2,1)}) %all-gather.8.cloned.1.call-update) | async-done | bytes 3145744 | tf_op jit(solution)/shard_map/all_gather | solution.py:541
  269.4 9.2 %multiply_convert_fusion.1 = (bf16[1024,768]{1,0:T(8,128)(2,1)S(1)}, bf16[1024,768]{1,0:T(8,128)(2,1)S(1)}) fusion(f32[1024,768]{1,0:T(8,128)} %get-tuple-element.58, f32[1024,768]{1,0:T(8,128)} %get-tuple-element.57, bf16[1024,2048]{1,0:T(8,128)(2,1)} %bitcast.57, bf16[2048,768]{1,0:T(8,128)(2,1)} %all-gather.8.cloned.1.call-done.down), kind=kOutput, calls=%fused_computation.5 | convolution fusion | flops 3231449088 | bytes 16777216 | tf_op jit(solution)/shard_map/dot_general | solution.py:35
  280.2 9.3 %convolution_convert_fusion = bf16[2048,1536]{1,0:T(8,128)(2,1)} fusion(bf16[1024,2048]{1,0:T(8,128)(2,1)S(1)} %bitcast.69, bf16[1024,768]{1,0:T(8,128)(2,1)S(1)} %get-tuple-element.108, bf16[1024,768]{1,0:T(8,128)(2,1)S(1)} %get-tuple-element.107), kind=kOutput, calls=%fused_computation | convolution fusion | flops 6451888128 | bytes 13631488 | tf_op jit(solution)/shard_map/dot_general | solution.py:39
  289.6 2.2 pad_maximum_fusion.d_gate_up
  291.9 67.3 %shard_map.241 = (f32[128,2048]{1,0:T(8,128)S(1)}, bf16[8,128,2048]{2,1,0:T(8,128)(2,1)S(1)}) custom-call(bf16[1024,1536]{1,0:T(8,128)(2,1)S(1)} %pad_maximum_fusion.d_gate_up, bf16[2048,1536]{1,0:T(8,128)(2,1)} %all-gather.6.cloned.1.call-done.gate_up, f32[128,2048]{1,0:T(8,128)S(1)} %copy-done.17, bf16[128,2048]{1,0:T(8,128)(2,1)S(1)} %copy-done.13), custom_call_target="tpu_custom_call" | custom-call | tf_op jit(solution)/shard_map/pallas_call | solution.py:234
  362.2 9.4 %heads.1 = (bf16[1024,512]{1,0:T(8,128)(2,1)S(1)}, f32[2,128]{1,0:T(2,128)S(1)}) custom-call(f32[1024,512]{1,0:T(8,128)S(1)} %copy-done.4, f32[128,128]{1,0:T(8,128)S(1)} %get-tuple-element.135.cosine, f32[128,128]{1,0:T(8,128)S(1)} %get-tuple-element.136.sine, s32[1024,128]{1,0:T(8,128)S(1)} %copy-done.11, f32[2,128]{1,0:T(2,128)S(1)} %pad_maximum_fusion.4.gains, ...), custom_call_target="tpu_custom_call" | custom-call | tf_op jit(solution)/shard_map/heads/pallas_call | solution.py:669
  371.6 2.4 convolution_convert_fusion.2
  374.1 2.1 pad_maximum_fusion.1
  381.3 1.9 copy-done.19
  385.6 67.7 %shard_map.242 = (bf16[2,128,2048]{2,1,0:T(8,128)(2,1)S(1)}, bf16[128,2048]{1,0:T(8,128)(2,1)S(1)}, f32[2,128]{1,0:T(2,128)S(1)}) custom-call(bf16[1024,512]{1,0:T(8,128)(2,1)S(1)} %copy-done.24, bf16[2048,768]{1,0:T(8,128)(2,1)S(1)} %copy-done.2, bf16[1024,768]{1,0:T(8,128)(2,1)S(1)} %copy-done.9, bf16[2048,768]{1,0:T(8,128)(2,1)S(1)} %copy-done.19, ...), custom_call_target="tpu_custom_call" | custom-call | tf_op jit(solution)/shard_map/pallas_call | solution.py:234
  454.6 1.6 bitcast_convert_fusion
  457.7 39.3 %reduce-scatter.6.cloned.1.call-done = bf16[512,768]{1,0:T(8,128)(2,1)} async-done(((bf16[2048,768]{1,0:T(8,128)(2,1)}), bf16[512,768]{1,0:T(8,128)(2,1)}) %reduce-scatter.6.cloned.1.call-update) | async-done | bytes 786448 | tf_op jit(solution)/shard_map/reduce_scatter | solution.py:545
  497.0 112.9 %reduce-scatter.4.cloned.1.call-done = bf16[512,1536]{1,0:T(8,128)(2,1)} async-done(((bf16[2048,1536]{1,0:T(8,128)(2,1)}), bf16[512,1536]{1,0:T(8,128)(2,1)}) %reduce-scatter.4.cloned.1.call-update) | async-done | bytes 1572880 | tf_op jit(solution)/shard_map/reduce_scatter | solution.py:545
  612.4 28.9 %shard_map.243 = (bf16[128,3072]{1,0:T(8,128)(2,1)S(1)}, bf16[128,3072]{1,0:T(8,128)(2,1)S(1)}, bf16[128,3072]{1,0:T(8,128)(2,1)S(1)}, bf16[2,128,2048]{2,1,0:T(8,128)(2,1)S(1)}) custom-call(bf16[4,128,1536]{2,1,0:T(8,128)(2,1)S(1)} %bitcast.61, bf16[4,128,768]{2,1,0:T(8,128)(2,1)S(1)} %bitcast.64, bf16[128,2048]{1,0:T(8,128)(2,1)S(1)} %copy-done.27), custom_call_target="tpu_custom_call" | custom-call | tf_op jit(solution)/shard_map/pallas_call | solution.py:234
  641.3 11.8 %shard_map.244 = (bf16[128,1024]{1,0:T(8,128)(2,1)S(1)}, bf16[128,512]{1,0:T(8,128)(2,1)S(1)}, bf16[128,512]{1,0:T(8,128)(2,1)S(1)}, bf16[128,1024]{1,0:T(8,128)(2,1)S(1)}) custom-call(bf16[4,128,768]{2,1,0:T(8,128)(2,1)S(1)} %bitcast.59), custom_call_target="tpu_custom_call" | custom-call | tf_op jit(solution)/shard_map/pallas_call | solution.py:234
  657.5 2.5 convert_multiply_fusion
  661.1 3.0 copy.40
  665.5 2.2 collective-permute-done.1
  (139 shorter events, 36.7 us)
Async XLA Ops:
  7.2 19.1 %copy-start = (bf16[256,2048]{1,0:T(8,128)(2,1)S(1)}, bf16[256,2048]{1,0:T(8,128)(2,1)}, u32[]{:S(2)}) copy-start(bf16[256,2048]{1,0:T(8,128)(2,1)} %param.14) | copy-start | bytes 3145732
  7.2 20.8 %copy-start.34 = (bf16[128,3072]{1,0:T(8,128)(2,1)S(1)}, bf16[128,3072]{1,0:T(8,128)(2,1)}, u32[]{:S(2)}) copy-start(bf16[128,3072]{1,0:T(8,128)(2,1)} %param.26) | copy-start | bytes 2359300
  7.2 20.8 %copy-start.36 = (bf16[128,3072]{1,0:T(8,128)(2,1)S(1)}, bf16[128,3072]{1,0:T(8,128)(2,1)}, u32[]{:S(2)}) copy-start(bf16[128,3072]{1,0:T(8,128)(2,1)} %param.25) | copy-start | bytes 2359300
  7.2 20.8 %copy-start.45 = (f32[128]{0:T(128)S(1)}, f32[128]{0:T(128)}, u32[]{:S(2)}) copy-start(f32[128]{0:T(128)} %param.24) | copy-start | bytes 1540
  7.2 83.3 %all-gather.4.cloned.1.call-start = ((), (), s32[]{:S(2)}) async-start(), calls=%async_computation.3 | async-start | bytes 3932160 | tf_op jit(solution)/shard_map/all_gather | solution.py:541
  26.2 179.9 %all-gather.6.cloned.1.call-start = ((), (), s32[]{:S(2)}) async-start(), calls=%async_computation.4 | async-start | bytes 7864320 | tf_op jit(solution)/shard_map/all_gather | solution.py:541
  26.3 51.4 %copy-start.5 = (bf16[128,2048]{1,0:T(8,128)(2,1)}, bf16[128,2048]{1,0:T(8,128)(2,1)S(1)}, u32[]{:S(2)}) copy-start(bf16[128,2048]{1,0:T(8,128)(2,1)S(1)} %dynamic-slice_bitcast_fusion.1.tokens) | copy-start | bytes 1572868
  28.4 52.6 %copy-start.46 = (f32[128]{0:T(128)S(1)}, f32[128]{0:T(128)}, u32[]{:S(2)}) copy-start(f32[128]{0:T(128)} %param.23) | copy-start | bytes 1540
  28.4 52.6 %copy-start.47 = (f32[128]{0:T(128)S(1)}, f32[128]{0:T(128)}, u32[]{:S(2)}) copy-start(f32[128]{0:T(128)} %param.22) | copy-start | bytes 1540
  28.4 53.0 %copy-start.43 = (bf16[256,2048]{1,0:T(8,128)(2,1)S(1)}, bf16[256,2048]{1,0:T(8,128)(2,1)}, u32[]{:S(2)}) copy-start(bf16[256,2048]{1,0:T(8,128)(2,1)} %param.15) | copy-start | bytes 3145732
  79.8 189.6 %all-gather.8.cloned.1.call-start = ((), (), s32[]{:S(2)}) async-start(), calls=%async_computation.5 | async-start | bytes 3932160 | tf_op jit(solution)/shard_map/all_gather | solution.py:541
  80.5 375.8 %reduce-scatter.8.cloned.1.call-start = ((), (), s32[]{:S(2)}) async-start(), calls=%async_computation.8 | async-start | bytes 3932160 | tf_op jit(solution)/shard_map/reduce_scatter | solution.py:545
  90.6 5.5 copy-start.2
  90.6 5.5 copy-start.6
  95.9 59.5 %copy-start.3 = (f32[1024,512]{1,0:T(8,128)}, f32[1024,512]{1,0:T(8,128)S(1)}, u32[]{:S(2)}) copy-start(f32[1024,512]{1,0:T(8,128)S(1)} %fusion.qkv) | copy-start | bytes 6291460
  96.1 59.3 %copy-start.10 = (s32[1024,128]{1,0:T(8,128)}, s32[1024,128]{1,0:T(8,128)S(1)}, u32[]{:S(2)}) copy-start(s32[1024,128]{1,0:T(8,128)S(1)} %broadcast_in_dim.12.start) | copy-start | bytes 1572868
  96.1 63.1 %copy-start.12 = (bf16[128,2048]{1,0:T(8,128)(2,1)S(1)}, bf16[128,2048]{1,0:T(8,128)(2,1)}, u32[]{:S(2)}) copy-start(bf16[128,2048]{1,0:T(8,128)(2,1)} %dynamic-slice_bitcast_fusion.grads) | copy-start | bytes 1572868
  269.4 10.9 %copy-start.31 = (bf16[8,128,2048]{2,1,0:T(8,128)(2,1)S(1)}, bf16[8,128,2048]{2,1,0:T(8,128)(2,1)}, u32[]{:S(2)}) copy-start(bf16[8,128,2048]{2,1,0:T(8,128)(2,1)} %copy-done.30) | copy-start | bytes 12582916
  291.9 67.3 %copy-start.33 = (bf16[1024,256]{1,0:T(8,128)(2,1)S(1)}, bf16[1024,256]{1,0:T(8,128)(2,1)}, u32[]{:S(2)}) copy-start(bf16[1024,256]{1,0:T(8,128)(2,1)} %copy-done.32) | copy-start | bytes 1572868
  360.6 11.1 %copy-start.29 = (bf16[8,128,2048]{2,1,0:T(8,128)(2,1)S(1)}, bf16[8,128,2048]{2,1,0:T(8,128)(2,1)}, u32[]{:S(2)}) copy-start(bf16[8,128,2048]{2,1,0:T(8,128)(2,1)} %copy-done.28) | copy-start | bytes 12582916
  376.2 120.8 %reduce-scatter.6.cloned.1.call-start = ((), (), s32[]{:S(2)}) async-start(), calls=%async_computation.7 | async-start | bytes 3932160 | tf_op jit(solution)/shard_map/reduce_scatter | solution.py:545
  376.8 233.1 %reduce-scatter.4.cloned.1.call-start = ((), (), s32[]{:S(2)}) async-start(), calls=%async_computation.6 | async-start | bytes 7864320 | tf_op jit(solution)/shard_map/reduce_scatter | solution.py:545
  454.1 155.8 %copy-start.27 = (bf16[128,2048]{1,0:T(8,128)(2,1)S(1)}, bf16[128,2048]{1,0:T(8,128)(2,1)}, u32[]{:S(2)}) copy-start(bf16[128,2048]{1,0:T(8,128)(2,1)} %copy-done.26) | copy-start | bytes 1572868
  456.2 196.9 %copy-start.40 = (bf16[128,1024]{1,0:T(8,128)(2,1)S(1)}, bf16[128,1024]{1,0:T(8,128)(2,1)}, u32[]{:S(2)}) copy-start(bf16[128,1024]{1,0:T(8,128)(2,1)} %param.18) | copy-start | bytes 786436
  456.2 196.9 %copy-start.44 = (f32[128]{0:T(128)S(1)}, f32[128]{0:T(128)}, u32[]{:S(2)}) copy-start(f32[128]{0:T(128)} %param.17) | copy-start | bytes 1540
  456.2 197.8 %copy-start.41 = (bf16[128,512]{1,0:T(8,128)(2,1)S(1)}, bf16[128,512]{1,0:T(8,128)(2,1)}, u32[]{:S(2)}) copy-start(bf16[128,512]{1,0:T(8,128)(2,1)} %param.20) | copy-start | bytes 393220
  456.2 197.8 %copy-start.42 = (bf16[128,512]{1,0:T(8,128)(2,1)S(1)}, bf16[128,512]{1,0:T(8,128)(2,1)}, u32[]{:S(2)}) copy-start(bf16[128,512]{1,0:T(8,128)(2,1)} %param.19) | copy-start | bytes 393220
  641.3 16.2 %copy-start.35 = (bf16[128,3072]{1,0:T(8,128)(2,1)S(1)}, bf16[128,3072]{1,0:T(8,128)(2,1)}, u32[]{:S(2)}) copy-start(bf16[128,3072]{1,0:T(8,128)(2,1)} %param.26) | copy-start | bytes 2359300
  641.3 16.2 %copy-start.37 = (bf16[128,3072]{1,0:T(8,128)(2,1)S(1)}, bf16[128,3072]{1,0:T(8,128)(2,1)}, u32[]{:S(2)}) copy-start(bf16[128,3072]{1,0:T(8,128)(2,1)} %param.25) | copy-start | bytes 2359300
  655.0 10.0 %collective-permute-start = (f32[1,128]{1,0:T(1,128)S(1)}, f32[1,128]{1,0:T(1,128)S(1)}, u32[]{:S(2)}, u32[]{:S(2)}) collective-permute-start(f32[1,128]{1,0:T(1,128)S(1)} %add_bitcast_fusion.3), channel_id=1, source_target_pairs={{0,1},{1,0},{2,3},{3,2},{4,5},{5,4},{6,7},{7,6},{8,9},{9,8},{10,11... | collective-permute-start | bytes 1544 | tf_op jit(solution)/shard_map/ppermute | solution.py:536
  660.1 9.1 %copy-start.1 = (bf16[256,2048]{1,0:T(8,128)(2,1)S(1)}, bf16[256,2048]{1,0:T(8,128)(2,1)}, u32[]{:S(2)}) copy-start(bf16[256,2048]{1,0:T(8,128)(2,1)} %param.14) | copy-start | bytes 3145732
  664.1 3.6 collective-permute-start.1
  (24 other events, 38.7 us)
Sparse Core Ops, SparseCore 0:
  26.4 64.1 all-gather.3
  92.1 113.9 all-gather.5
  207.7 61.6 all-gather.7
  376.4 58.0 reduce-scatter.7
  436.6 60.3 reduce-scatter.5
  499.2 110.6 reduce-scatter.3

commit v2 on v1

--- a/solution.py
+++ b/solution.py
@@ -4,6 +4,7 @@
 import jax.numpy as jnp
 from jax import lax
 from jax.experimental import pallas as pl
+from jax.experimental.layout import Layout, with_layout_constraint
 from jax.experimental.pallas import tpu as pltpu
 from jax.sharding import Mesh
 from jax.sharding import PartitionSpec as P
@@ -287,11 +288,26 @@
     return start_all(copies)
 
 
-def enter_kernel(query, key, value, output, segments, slabs, segments_all, *sems):
+def enter_kernel(query, key, value, output, slabs, *sems):
     greet(square)
     size, other = query.shape[1] // 4, key.shape[1] // 4
     targets = [(slabs, at) for at in (0, size, size + other, size + 2 * other)]
-    copies = spread_start((query, key, value, output), targets, sems[:2])
+    wait_all(spread_start((query, key, value, output), targets, sems))
+
+
+def tokens_kernel(tokens, gate, up, down, segments, inputs_all, gate_up_slabs, down_slabs,
+                  segments_all, *sems):
+    greet(square + [("y", 1)])
+
+    def norm(row):
+        normed, _ = normalize(tokens[row].astype(f32))
+        inputs_all[0, row] = normed.astype(bf16)
+
+    over_rows(tokens.shape[0], norm)
+    hidden = gate.shape[1] // 4
+    targets = ((gate_up_slabs, 0), (gate_up_slabs, hidden), (down_slabs, 0))
+    gather = gather_start(inputs_all, sems[:2])
+    copies = spread_start((gate, up, down), targets, sems[2:4])
     segments_all[0] = segments[...]
     copies += start_all(
         [
@@ -299,27 +315,12 @@
                 square_id(step),
                 segments,
                 segments_all.at[step // 2 + step % 2 * 2],
-                sems[2:],
+                sems[4:],
                 step,
             )
             for step in (1, 2, 3)
         ]
     )
-    wait_all(copies)
-
-
-def tokens_kernel(tokens, gate, up, down, inputs_all, gate_up_slabs, down_slabs, *sems):
-    greet(square + [("y", 1)])
-
-    def norm(row):
-        normed, _ = normalize(tokens[row].astype(f32))
-        inputs_all[0, row] = normed.astype(bf16)
-
-    over_rows(tokens.shape[0], norm)
-    hidden = gate.shape[1] // 4
-    targets = ((gate_up_slabs, 0), (gate_up_slabs, hidden), (down_slabs, 0))
-    gather = gather_start(inputs_all, sems[:2])
-    copies = spread_start((gate, up, down), targets, sems[2:])
     gather_finish(*gather)
     wait_all(copies)
 
@@ -582,33 +583,34 @@
     def scatter_shapes():
         return scatter_scratch(block_rows, width)
 
+    attention_slabs = call(
+        enter_kernel,
+        1,
+        array(bf16, 4, rows_here, qkv_size + output_size),
+        sem_pair(16),
+        *(scaled(w, gain_one) for w in (query_weight, key_weight, value_weight)),
+        output_weight.T,
+    )
+    attention_all = fetch(attention_slabs)
+    qkv_weight = attention_all[:, :qkv_size]
+    token_own, segments, _ = lax.optimization_barrier((token_own, segments, attention_slabs))
     pairs = segments.reshape(2, -1, rows)
     pairs = jnp.where(mine == 0, pairs, pairs[::-1]).reshape(blocks, rows)
-    attention_slabs, segments_all = call(
-        enter_kernel,
-        1,
-        (array(bf16, 4, rows_here, qkv_size + output_size), array(jnp.int32, 4, blocks, rows)),
-        sem_pair(16) + sem_pair(4),
-        *(scaled(w, gain_one) for w in (query_weight, key_weight, value_weight)),
-        output_weight.T,
-        pairs,
-    )
-    attention_all = fetch(attention_slabs)
-    qkv_weight = attention_all[:, :qkv_size]
-    token_own, _ = lax.optimization_barrier((token_own, segments_all))
-    input_one, gate_up_slabs, down_slabs = call(
+    input_one, gate_up_slabs, down_slabs, segments_all = call(
         tokens_kernel,
         2,
         (
             everyone,
             array(bf16, 4, rows_here, 2 * hidden_size),
             array(bf16, 4, rows_here, hidden_size),
+            array(jnp.int32, 4, blocks, rows),
         ),
-        sem_pair(14) + sem_pair(12),
+        sem_pair(14) + sem_pair(12) + sem_pair(4),
         token_own,
         scaled(gate_weight, gain_two),
         scaled(up_weight, gain_two),
         down_weight.T,
+        pairs,
     )
     input_one = input_one.reshape(-1, width)
     gate_up_all = fetch(gate_up_slabs)
@@ -678,6 +680,7 @@
         [dot_tn(input_one, d_qkv).astype(bf16), grad_output], axis=1
     )
     d_qkv, grad_attention = lax.optimization_barrier((d_qkv, grad_attention))
+    grad_attention = with_layout_constraint(grad_attention, Layout((0, 1)))
     grad_attention = give_back(grad_attention)
     stages = 3 + depth.bit_length() - 1
     grad_tokens, mixed_own, head_gains = call(

time: 677 us -> 545 us (0.81)
  waiting for transfers between devices: 231 us -> 95.4 us
    reduce_scatter x3, waiting for transfers between devices: 152 us -> 15.9 us  [give_back(): summed_rows = lax.psum_scatter(grads, 'z', scatter_dimension=0, tiled=True)]
    unnamed x101 -> x99, local copies, waits for them, and re-layouts: 30.4 us -> 38.5 us
  transfers between devices with their start and end apart: 8 -> 8, of which waited for: 6 -> 5; matrix products, arithmetic and copies ran while one was open for 6% -> 12% of each run, Pallas kernels for 29% -> 56%
where the time goes in v2:
time: 545 us; the launch traced here: 544 us
  Pallas kernels  329 us (60%)
  waiting for transfers between devices  95.4 us (18%)
  matrix products  44.2 us (8%)
  local copies, waits for them, and re-layouts  39.4 us (7%)
  other arithmetic  19 us (3%)
  between operations  14.7 us (3%)
    pallas_call x8, Pallas kernels, call(): pl.pallas_call(kernel, out_shape=outputs, in_specs=[pl.BlockSpec(memory_s...  319 us
    all_gather x3, waiting for transfers between devices, fetch(): return lax.all_gather(spread.reshape(-1, columns), 'z', axis=0, tiled=True)  76.3 us
    unnamed x99, local copies, waits for them, and re-layouts  38.5 us
    dot_general x4, matrix products, dot(): return jnp.dot(left, right, preferred_element_type=f32)  26.1 us
    dot_general x4, matrix products, dot_tn(): lax.dot_general(left, right, (((0,), (0,)), ((), ())), preferred_element_...  18.1 us
    reduce_scatter x3, waiting for transfers between devices, give_back(): summed_rows = lax.psum_scatter(grads, 'z', scatter_dimension=0, tiled=True)  15.9 us
  transfers between devices with their start and end apart: 8, of which 5 were waited for; matrix products, arithmetic and copies ran while one was open for 12% of the time, Pallas kernels for 56%

profile of v2, /device:TPU:0, one launch (start us, length us, event | category | flops | bytes accessed | tf_op | source)
XLA Modules:
  0.0 544.0 jit_solution(2413003782391498793)
XLA Ops:
  10.7 14.0 %shard_map.237 = bf16[4,128,768]{2,1,0:T(8,128)(2,1)} custom-call(bf16[128,1024]{1,0:T(8,128)(2,1)S(1)} %fusion.7.query, bf16[128,512]{1,0:T(8,128)(2,1)S(1)} %get-tuple-element.134.key, bf16[128,512]{1,0:T(8,128)(2,1)S(1)} %get-tuple-element.133.value, bf16[128,1024]{1,0:T(8,128)(2,1)S(1)} %bitcast.62), custom_call_target="tpu_custom_call" | custom-call | tf_op jit(solution)/shard_map/pallas_call | solution.py:235
  27.0 49.6 %shard_map.238 = (bf16[8,128,2048]{2,1,0:T(8,128)(2,1)S(1)}, bf16[4,128,1536]{2,1,0:T(8,128)(2,1)}, bf16[4,128,768]{2,1,0:T(8,128)(2,1)}, s32[4,2,128]{2,1,0:T(2,128)S(1)}) custom-call(bf16[128,2048]{1,0:T(8,128)(2,1)S(1)} %dynamic-slice_bitcast_fusion.1.tokens, bf16[128,3072]{1,0:T(8,128)(2,1)S(1)} %get-tuple-element.132.gate, ...), custom_call_target="tpu_custom_call" | custom-call | tf_op jit(solution)/shard_map/pallas_call | solution.py:235
  76.6 2.0 copy-done.31
  80.4 9.3 %all-gather.4.cloned.1.call-done.output.weights = bf16[2048,768]{1,0:T(8,128)(2,1)} async-done(((bf16[512,768]{1,0:T(8,128)(2,1)}), bf16[2048,768]{1,0:T(8,128)(2,1)}) %all-gather.4.cloned.1.call-update) | async-done | bytes 3145744 | tf_op jit(solution)/shard_map/all_gather | solution.py:542
  89.8 5.3 fusion.qkv
  95.3 59.2 %shard_map.239 = (bf16[1024,256]{1,0:T(8,128)(2,1)S(1)}, f32[128,2048]{1,0:T(8,128)S(1)}, bf16[8,128,2048]{2,1,0:T(8,128)(2,1)S(1)}) custom-call(f32[1024,512]{1,0:T(8,128)S(1)} %fusion.qkv, f32[128,128]{1,0:T(8,128)S(1)} %get-tuple-element.135.cosine, f32[128,128]{1,0:T(8,128)S(1)} %get-tuple-element.136.sine, s32[1024,128]{1,0:T(8,128)S(1)} %broadcast_in_dim.12.start, ...), custom_call_target="tpu_custom_call" | custom-call | tf_op jit(solution)/shard_map/pallas_call | solution.py:235
  156.4 2.1 copy-done.33
  158.5 22.0 %shard_map.240 = bf16[8,128,2048]{2,1,0:T(8,128)(2,1)S(1)} custom-call(bf16[128,2048]{1,0:T(8,128)(2,1)S(1)} %dynamic-slice_bitcast_fusion.grads), custom_call_target="tpu_custom_call" | custom-call | tf_op jit(solution)/shard_map/pallas_call | solution.py:235
  180.5 2.1 copy-done.14
  182.6 22.8 %all-gather.6.cloned.1.call-done.gate_up = bf16[2048,1536]{1,0:T(8,128)(2,1)} async-done(((bf16[512,1536]{1,0:T(8,128)(2,1)}), bf16[2048,1536]{1,0:T(8,128)(2,1)}) %all-gather.6.cloned.1.call-update) | async-done | bytes 6291472 | tf_op jit(solution)/shard_map/all_gather | solution.py:542
  205.4 10.0 %fusion.15 = f32[1024,1536]{1,0:T(8,128)S(1)} fusion(bf16[1024,2048]{1,0:T(8,128)(2,1)} %bitcast.68, bf16[2048,1536]{1,0:T(8,128)(2,1)} %all-gather.6.cloned.1.call-done.gate_up), kind=kOutput, calls=%fused_computation.63 | convolution fusion | flops 6442450944 | bytes 16777216 | tf_op jit(solution)/shard_map/dot_general | solution.py:36
  215.4 2.7 fusion.14
  218.1 4.9 convolution_convert_fusion.1
  224.4 44.2 %all-gather.8.cloned.1.call-done.down = bf16[2048,768]{1,0:T(8,128)(2,1)} async-done(((bf16[512,768]{1,0:T(8,128)(2,1)}), bf16[2048,768]{1,0:T(8,128)(2,1)}) %all-gather.8.cloned.1.call-update) | async-done | bytes 3145744 | tf_op jit(solution)/shard_map/all_gather | solution.py:542
  268.6 8.2 %multiply_convert_fusion.1 = (bf16[1024,768]{1,0:T(8,128)(2,1)S(1)}, bf16[1024,768]{1,0:T(8,128)(2,1)S(1)}) fusion(f32[1024,768]{1,0:T(8,128)} %get-tuple-element.58, f32[1024,768]{1,0:T(8,128)S(1)} %get-tuple-element.57, bf16[1024,2048]{1,0:T(8,128)(2,1)} %bitcast.57, bf16[2048,768]{1,0:T(8,128)(2,1)} %all-gather.8.cloned.1.call-done.down), kind=kOutput, calls=%fused_computation.5 | convolution fusion | flops 3231449088 | bytes 16777216 | tf_op jit(solution)/shard_map/dot_general | solution.py:36
  277.0 1.9 copy-done.34
  278.9 9.4 %convolution_convert_fusion = bf16[2048,1536]{1,0:T(8,128)(2,1)} fusion(bf16[1024,2048]{1,0:T(8,128)(2,1)S(1)} %bitcast.69, bf16[1024,768]{1,0:T(8,128)(2,1)S(1)} %get-tuple-element.108, bf16[1024,768]{1,0:T(8,128)(2,1)S(1)} %get-tuple-element.107), kind=kOutput, calls=%fused_computation | convolution fusion | flops 6451888128 | bytes 13631488 | tf_op jit(solution)/shard_map/dot_general | solution.py:40
  290.9 67.3 %shard_map.241 = (f32[128,2048]{1,0:T(8,128)S(1)}, bf16[8,128,2048]{2,1,0:T(8,128)(2,1)S(1)}) custom-call(bf16[1024,1536]{1,0:T(8,128)(2,1)S(1)} %pad_maximum_fusion.d_gate_up, bf16[2048,1536]{1,0:T(8,128)(2,1)} %all-gather.6.cloned.1.call-done.gate_up, f32[128,2048]{1,0:T(8,128)S(1)} %copy-done.17, bf16[128,2048]{1,0:T(8,128)(2,1)S(1)} %copy-done.13), custom_call_target="tpu_custom_call" | custom-call | tf_op jit(solution)/shard_map/pallas_call | solution.py:235
  359.1 2.6 convolution_convert_fusion.4.d_attended
  361.8 9.4 %heads.1 = (bf16[1024,512]{1,0:T(8,128)(2,1)S(1)}, f32[2,128]{1,0:T(2,128)S(1)}) custom-call(f32[1024,512]{1,0:T(8,128)S(1)} %copy-done.5, f32[128,128]{1,0:T(8,128)S(1)} %get-tuple-element.135.cosine, f32[128,128]{1,0:T(8,128)S(1)} %get-tuple-element.136.sine, s32[1024,128]{1,0:T(8,128)S(1)} %copy-done.11, f32[2,128]{1,0:T(2,128)S(1)} %pad_maximum_fusion.4.gains, ...), custom_call_target="tpu_custom_call" | custom-call | tf_op jit(solution)/shard_map/heads/pallas_call | solution.py:671
  373.8 2.4 convolution_convert_fusion.2
  376.2 2.0 pad_maximum_fusion.1
  378.2 1.9 copy-done.3
  383.8 1.9 copy-done.19
  388.1 66.8 %shard_map.242 = (bf16[2,128,2048]{2,1,0:T(8,128)(2,1)S(1)}, bf16[128,2048]{1,0:T(8,128)(2,1)S(1)}, f32[2,128]{1,0:T(2,128)S(1)}) custom-call(bf16[1024,512]{1,0:T(8,128)(2,1)S(1)} %copy-done.24, bf16[2048,768]{1,0:T(8,128)(2,1)S(1)} %copy-done.3, bf16[1024,768]{1,0:T(8,128)(2,1)S(1)} %copy-done.9, bf16[2048,768]{1,0:T(8,128)(2,1)S(1)} %copy-done.19, ...), custom_call_target="tpu_custom_call" | custom-call | tf_op jit(solution)/shard_map/pallas_call | solution.py:235
  460.5 28.6 %shard_map.243 = (bf16[128,3072]{1,0:T(8,128)(2,1)S(1)}, bf16[128,3072]{1,0:T(8,128)(2,1)S(1)}, bf16[128,3072]{1,0:T(8,128)(2,1)S(1)}, bf16[2,128,2048]{2,1,0:T(8,128)(2,1)S(1)}) custom-call(bf16[4,128,1536]{2,1,0:T(8,128)(2,1)S(1)} %bitcast.60, bf16[4,128,768]{2,1,0:T(8,128)(2,1)S(1)} %bitcast.64, bf16[128,2048]{1,0:T(8,128)(2,1)S(1)} %copy-done.30), custom_call_target="tpu_custom_call" | custom-call | tf_op jit(solution)/shard_map/pallas_call | solution.py:235
  489.9 15.9 %reduce-scatter.8.cloned.1.call-done = bf16[512,768]{1,0:T(8,128)(2,1)} async-done(((bf16[2048,768]{1,0:T(8,128)(2,1)}), bf16[512,768]{1,0:T(8,128)(2,1)}) %reduce-scatter.8.cloned.1.call-update) | async-done | bytes 786448 | tf_op jit(solution)/shard_map/reduce_scatter | solution.py:546
  507.0 11.7 %shard_map.244 = (bf16[128,1024]{1,0:T(8,128)(2,1)S(1)}, bf16[128,512]{1,0:T(8,128)(2,1)S(1)}, bf16[128,512]{1,0:T(8,128)(2,1)S(1)}, bf16[128,1024]{1,0:T(8,128)(2,1)S(1)}) custom-call(bf16[4,128,768]{2,1,0:T(8,128)(2,1)S(1)} %bitcast.63), custom_call_target="tpu_custom_call" | custom-call | tf_op jit(solution)/shard_map/pallas_call | solution.py:235
  519.6 1.8 convert_multiply_fusion.9
  524.3 3.7 convert_multiply_fusion
  529.1 3.0 copy.42
  533.2 2.5 collective-permute-done.1
  (136 shorter events, 38.0 us)
Async XLA Ops:
  7.2 17.6 %copy-start = (bf16[256,2048]{1,0:T(8,128)(2,1)S(1)}, bf16[256,2048]{1,0:T(8,128)(2,1)}, u32[]{:S(2)}) copy-start(bf16[256,2048]{1,0:T(8,128)(2,1)} %param.14) | copy-start | bytes 3145732
  7.2 17.7 %copy-start.43 = (s32[2,128]{1,0:T(2,128)S(1)}, s32[2,128]{1,0:T(2,128)}, u32[]{:S(2)}) copy-start(s32[2,128]{1,0:T(2,128)} %param.16) | copy-start | bytes 3076
  7.2 82.6 %all-gather.4.cloned.1.call-start = ((), (), s32[]{:S(2)}) async-start(), calls=%async_computation.3 | async-start | bytes 3932160 | tf_op jit(solution)/shard_map/all_gather | solution.py:542
  8.4 18.1 %copy-start.37 = (bf16[128,3072]{1,0:T(8,128)(2,1)S(1)}, bf16[128,3072]{1,0:T(8,128)(2,1)}, u32[]{:S(2)}) copy-start(bf16[128,3072]{1,0:T(8,128)(2,1)} %param.26) | copy-start | bytes 2359300
  8.4 18.1 %copy-start.38 = (bf16[128,3072]{1,0:T(8,128)(2,1)S(1)}, bf16[128,3072]{1,0:T(8,128)(2,1)}, u32[]{:S(2)}) copy-start(bf16[128,3072]{1,0:T(8,128)(2,1)} %param.25) | copy-start | bytes 2359300
  8.4 18.1 %copy-start.44 = (f32[128]{0:T(128)S(1)}, f32[128]{0:T(128)}, u32[]{:S(2)}) copy-start(f32[128]{0:T(128)} %param.24) | copy-start | bytes 1540
  24.8 180.6 %all-gather.6.cloned.1.call-start = ((), (), s32[]{:S(2)}) async-start(), calls=%async_computation.4 | async-start | bytes 7864320 | tf_op jit(solution)/shard_map/all_gather | solution.py:542
  24.9 70.4 %copy-start.6 = (bf16[128,2048]{1,0:T(8,128)(2,1)}, bf16[128,2048]{1,0:T(8,128)(2,1)S(1)}, u32[]{:S(2)}) copy-start(bf16[128,2048]{1,0:T(8,128)(2,1)S(1)} %dynamic-slice_bitcast_fusion.1.tokens) | copy-start | bytes 1572868
  27.0 52.9 %copy-start.45 = (f32[128]{0:T(128)S(1)}, f32[128]{0:T(128)}, u32[]{:S(2)}) copy-start(f32[128]{0:T(128)} %param.23) | copy-start | bytes 1540
  27.0 52.9 %copy-start.46 = (f32[128]{0:T(128)S(1)}, f32[128]{0:T(128)}, u32[]{:S(2)}) copy-start(f32[128]{0:T(128)} %param.22) | copy-start | bytes 1540
  27.0 53.3 %copy-start.41 = (bf16[256,2048]{1,0:T(8,128)(2,1)S(1)}, bf16[256,2048]{1,0:T(8,128)(2,1)}, u32[]{:S(2)}) copy-start(bf16[256,2048]{1,0:T(8,128)(2,1)} %param.15) | copy-start | bytes 3145732
  78.7 189.9 %all-gather.8.cloned.1.call-start = ((), (), s32[]{:S(2)}) async-start(), calls=%async_computation.5 | async-start | bytes 3932160 | tf_op jit(solution)/shard_map/all_gather | solution.py:542
  79.4 378.5 %reduce-scatter.6.cloned.1.call-start = ((), (), s32[]{:S(2)}) async-start(), calls=%async_computation.7 | async-start | bytes 3932160 | tf_op jit(solution)/shard_map/reduce_scatter | solution.py:546
  80.4 76.0 %copy-start.12 = (bf16[128,2048]{1,0:T(8,128)(2,1)}, bf16[128,2048]{1,0:T(8,128)(2,1)S(1)}, u32[]{:S(2)}) copy-start(bf16[128,2048]{1,0:T(8,128)(2,1)S(1)} %dynamic-slice_bitcast_fusion.grads) | copy-start | bytes 1572868
  89.8 5.6 %copy-start.2 = (bf16[2048,768]{1,0:T(8,128)(2,1)S(1)}, bf16[2048,768]{1,0:T(8,128)(2,1)}, u32[]{:S(2)}) copy-start(bf16[2048,768]{1,0:T(8,128)(2,1)} %all-gather.4.cloned.1.call-done.output.weights) | copy-start | bytes 9437188
  95.1 59.5 %copy-start.4 = (f32[1024,512]{1,0:T(8,128)}, f32[1024,512]{1,0:T(8,128)S(1)}, u32[]{:S(2)}) copy-start(f32[1024,512]{1,0:T(8,128)S(1)} %fusion.qkv) | copy-start | bytes 6291460
  95.3 59.3 %copy-start.10 = (s32[1024,128]{1,0:T(8,128)}, s32[1024,128]{1,0:T(8,128)S(1)}, u32[]{:S(2)}) copy-start(s32[1024,128]{1,0:T(8,128)S(1)} %broadcast_in_dim.12.start) | copy-start | bytes 1572868
  215.4 2.7 copy-start.15
  224.2 233.7 %reduce-scatter.4.cloned.1.call-start = ((), (), s32[]{:S(2)}) async-start(), calls=%async_computation.6 | async-start | bytes 7864320 | tf_op jit(solution)/shard_map/reduce_scatter | solution.py:546
  276.7 2.2 copy-start.34
  288.3 217.5 %reduce-scatter.8.cloned.1.call-start = ((), (), s32[]{:S(2)}) async-start(), calls=%async_computation.8 | async-start | bytes 3932160 | tf_op jit(solution)/shard_map/reduce_scatter | solution.py:546
  359.1 2.6 copy-start.5
  359.1 2.6 copy-start.11
  361.8 9.4 %copy-start.36 = (bf16[1024,256]{1,0:T(8,128)(2,1)S(1)}, bf16[1024,256]{1,0:T(8,128)(2,1)}, u32[]{:S(2)}) copy-start(bf16[1024,256]{1,0:T(8,128)(2,1)} %copy-done.35) | copy-start | bytes 1572868
  371.2 2.6 copy-start.32
  456.3 62.4 %copy-start.39 = (bf16[128,1024]{1,0:T(8,128)(2,1)S(1)}, bf16[128,1024]{1,0:T(8,128)(2,1)}, u32[]{:S(2)}) copy-start(bf16[128,1024]{1,0:T(8,128)(2,1)} %param.18) | copy-start | bytes 786436
  456.3 62.4 %copy-start.42 = (f32[128]{0:T(128)S(1)}, f32[128]{0:T(128)}, u32[]{:S(2)}) copy-start(f32[128]{0:T(128)} %param.17) | copy-start | bytes 1540
  456.3 63.3 %copy-start.40 = (bf16[128,512]{1,0:T(8,128)(2,1)S(1)}, bf16[128,512]{1,0:T(8,128)(2,1)}, u32[]{:S(2)}) copy-start(bf16[128,512]{1,0:T(8,128)(2,1)} %param.20) | copy-start | bytes 393220
  507.0 17.4 %copy-start.28 = (bf16[128,3072]{1,0:T(8,128)(2,1)S(1)}, bf16[128,3072]{1,0:T(8,128)(2,1)}, u32[]{:S(2)}) copy-start(bf16[128,3072]{1,0:T(8,128)(2,1)} %copy-done.27) | copy-start | bytes 2359300
  521.5 11.2 %collective-permute-start = (f32[1,128]{1,0:T(1,128)S(1)}, f32[1,128]{1,0:T(1,128)S(1)}, u32[]{:S(2)}, u32[]{:S(2)}) collective-permute-start(f32[1,128]{1,0:T(1,128)S(1)} %add_bitcast_fusion.3), channel_id=1, source_target_pairs={{0,1},{1,0},{2,3},{3,2},{4,5},{5,4},{6,7},{7,6},{8,9},{9,8},{10,11... | collective-permute-start | bytes 1544 | tf_op jit(solution)/shard_map/ppermute | solution.py:537
  528.1 9.1 %copy-start.1 = (bf16[256,2048]{1,0:T(8,128)(2,1)S(1)}, bf16[256,2048]{1,0:T(8,128)(2,1)}, u32[]{:S(2)}) copy-start(bf16[256,2048]{1,0:T(8,128)(2,1)} %param.14) | copy-start | bytes 3145732
  532.1 3.6 collective-permute-start.1
  (23 other events, 31.2 us)
Sparse Core Ops, SparseCore 0:
  24.9 64.8 all-gather.3
  91.3 113.9 all-gather.5
  206.9 61.6 all-gather.7
  270.7 59.0 reduce-scatter.5
  332.0 110.7 reduce-scatter.3
  444.9 60.9 reduce-scatter.7
